TPU v7x, 32 devices: a whole 2x2x4 slice. The times are simulated.
32 devices in a mesh: job: 4 (over y, x), dp: 2 (over core), tp: 4 (over z).
Axes of the slice: x: 2, y: 2, z: 4, core: 2. Of those that a mesh axis runs over, the one named last changes fastest.
Arguments:
- partial_up: float32 [8, 768, 3072], P(('job', 'dp'), None, 'tp'), parts along dimension 0, may hold values from -0.875 to 0.875
- partial_down: float32 [8, 3072, 768], P(('job', 'dp'), 'tp'), parts along dimension 0, may hold values from -0.875 to 0.875
- partial_norm: float32 [8, 768], P(('job', 'dp')), parts along dimension 0, may hold values from -8 to 8
- partial_bias: float32 [8, 768], P(('job', 'dp')), parts along dimension 0, may hold values from -8 to 8
- master_up: float32 [3072, 3072], P(('job', 'dp'), 'tp'), parts along dimension 0, may hold values from -0.3125 to 0.3125
- master_down: float32 [12288, 768], P(('job', 'tp'), 'dp'), parts along dimension 0, may hold values from -0.15625 to 0.15625
- master_norm: float32 [3072], P(('job', 'dp')), parts along dimension 0, may hold values from 0.25 to 1.75
- master_bias: float32 [3072], P(('job', 'dp')), parts along dimension 0, may hold values from -3 to 3
- memory_up: float32 [3072, 3072], P(('job', 'dp'), 'tp'), parts along dimension 0, may hold values from -0.21875 to 0.21875
- memory_down: float32 [12288, 768], P(('job', 'tp'), 'dp'), parts along dimension 0, may hold values from -0.109375 to 0.109375
- memory_norm: float32 [3072], P(('job', 'dp')), parts along dimension 0, may hold values from -1.75 to 1.75
- memory_bias: float32 [3072], P(('job', 'dp')), parts along dimension 0, may hold values from -1.75 to 1.75
Outputs:
- compute_up: bfloat16 [3072, 3072], P('job', 'tp'), parts along dimension 0
- compute_down: bfloat16 [12288, 768], P(('job', 'tp')), parts along dimension 0
- compute_norm: bfloat16 [3072], P('job'), parts along dimension 0
- compute_bias: bfloat16 [3072], P('job'), parts along dimension 0
- stepped_up: float32 [3072, 3072], P(('job', 'dp'), 'tp'), parts along dimension 0
- stepped_down: float32 [12288, 768], P(('job', 'tp'), 'dp'), parts along dimension 0
- stepped_norm: float32 [3072], P(('job', 'dp')), parts along dimension 0
- stepped_bias: float32 [3072], P(('job', 'dp')), parts along dimension 0
- state_new_up: float32 [3072, 3072], P(('job', 'dp'), 'tp'), parts along dimension 0
- state_new_down: float32 [12288, 768], P(('job', 'tp'), 'dp'), parts along dimension 0
- state_new_norm: float32 [3072], P(('job', 'dp')), parts along dimension 0
- state_new_bias: float32 [3072], P(('job', 'dp')), parts along dimension 0
There are 4 independent parts, one for each index of `job`. A program takes and returns all parts, laid end to end along the dimension named above; each array names one. Nothing has to cross between parts.
All inputs are finite; a program needn't handle non-finite values.
Results may differ from a plain program's by a relative error of at most 0.001.
Values may be sent and summed in bfloat16 or wider, within the bound.
A program may use at most 64 MiB of HBM per device.

v0:
```python
import functools

import jax
import jax.numpy as jnp
from jax import lax
from jax.experimental import pallas as pl
from jax.experimental.pallas import tpu as pltpu
from jax.sharding import PartitionSpec as P

learn_rate = 0.4
hold_rate = 0.9


def on_device(
    partial_up,
    partial_down,
    partial_norm,
    partial_bias,
    master_up,
    master_down,
    master_norm,
    master_bias,
    memory_up,
    memory_down,
    memory_norm,
    memory_bias,
):
    mean_up, mean_down = (
        lax.psum_scatter(partial_up[0], "dp", scatter_dimension=0, tiled=True),
        lax.psum_scatter(partial_down[0], "dp", scatter_dimension=1, tiled=True),
    )
    whole_norm, whole_bias = lax.psum((partial_norm[0], partial_bias[0]), "dp")
    place = lax.axis_index("dp")
    mean_norm = lax.dynamic_slice_in_dim(
        whole_norm, place * master_norm.shape[0], master_norm.shape[0]
    )
    mean_bias = lax.dynamic_slice_in_dim(
        whole_bias, place * master_bias.shape[0], master_bias.shape[0]
    )
    mean_rate = lax.axis_size("dp") ** (-0.5)
    mean_up = mean_up * mean_rate
    mean_down = mean_down * mean_rate
    mean_norm = mean_norm * mean_rate
    mean_bias = mean_bias * mean_rate
    own_up, own_down, slope_up_norm, slope_down_norm = lax.psum(
        (
            jnp.sum(master_up * master_up, axis=1, keepdims=True),
            jnp.sum(master_down * master_down, axis=0, keepdims=True),
            jnp.sum(mean_up * mean_up, axis=1, keepdims=True),
            jnp.sum(mean_down * mean_down, axis=0, keepdims=True),
        ),
        "tp",
    )
    mean_up = mean_up * (jnp.sqrt(own_up) * lax.rsqrt(slope_up_norm + 1e-06))
    mean_down = mean_down * (jnp.sqrt(own_down) * lax.rsqrt(slope_down_norm + 1e-06))
    state_new_up = hold_rate * memory_up + mean_up
    stepped_up = master_up - learn_rate * state_new_up
    state_new_down = hold_rate * memory_down + mean_down
    stepped_down = master_down - learn_rate * state_new_down
    state_new_norm = hold_rate * memory_norm + mean_norm
    stepped_norm = master_norm - learn_rate * state_new_norm
    state_new_bias = hold_rate * memory_bias + mean_bias
    stepped_bias = master_bias - learn_rate * state_new_bias
    compute_up, compute_down, compute_norm, compute_bias = (
        lax.all_gather(stepped_up.astype(jnp.bfloat16), "dp", axis=0, tiled=True),
        lax.all_gather(stepped_down.astype(jnp.bfloat16), "dp", axis=1, tiled=True),
        lax.all_gather(stepped_norm.astype(jnp.bfloat16), "dp", axis=0, tiled=True),
        lax.all_gather(stepped_bias.astype(jnp.bfloat16), "dp", axis=0, tiled=True),
    )
    return (
        compute_up,
        compute_down,
        compute_norm,
        compute_bias,
        stepped_up,
        stepped_down,
        stepped_norm,
        stepped_bias,
        state_new_up,
        state_new_down,
        state_new_norm,
        state_new_bias,
    )


chunks = 4
pieces = 4
lanes = 128


def lane_sums(x):
    total = x[:, :lanes]
    for at in range(lanes, x.shape[1], lanes):
        total = total + x[:, at : at + lanes]
    return total


def exchange(
    pu, pd, pn, pb, mu_h, md_h, mn, mb, eu_h, ed_h, en, eb,
    cu, cd, cn, cb, su, sd, sn, sb, tu, td, tn, tb,
    own_u, own_d, give_u, give_d, got_u, got_d, mu, md, eu, ed, pn_v, pb_v, mn_v, mb_v, en_v, eb_v, vec, got_vec,
    sq_u, acc_d, stat_u, stat_d,
    load_sem, give_sem, part_send, part_recv, vec_sem, stat_send, stat_recv, out_send, out_recv,
):
    me = lax.axis_index("dp")
    peer = 1 - me
    here = lax.axis_index("tp")
    n = lax.axis_size("tp")
    rate = lax.axis_size("dp") ** (-0.5)
    rows, wide = mu.shape
    tall, cols = md.shape
    part_u, part_d = rows // chunks, tall // chunks

    def mine(size):
        return pl.ds(pl.multiple_of(me * size, size), size)

    def theirs(size):
        return pl.ds(pl.multiple_of(peer * size, size), size)

    barrier = pltpu.get_barrier_semaphore()
    pl.semaphore_signal(barrier, inc=1, device_id={"dp": peer})
    for step in range(1, n):
        pl.semaphore_signal(barrier, inc=1, device_id={"tp": lax.rem(here + step, n)})

    give = []
    for at in range(chunks):
        span = pl.ds(at * part_u, part_u)
        give.append(pltpu.make_async_copy(
            pu.at[pl.ds(pl.multiple_of(peer * rows + at * part_u, 8), part_u), :],
            give_u.at[span, :],
            give_sem.at[0, at],
        ))
    for at in range(chunks):
        span = pl.ds(at * part_d, part_d)
        give.append(pltpu.make_async_copy(
            pd.at[span, theirs(cols)], give_d.at[span, :], give_sem.at[1, at]
        ))
    loads = [
        pltpu.make_async_copy(source, target, load_sem.at[at])
        for at, (source, target) in enumerate((
            (mu_h, mu),
            (md_h, md),
            (pu.at[mine(rows), :], own_u),
            (pd.at[:, mine(cols)], own_d),
            (eu_h, eu),
            (ed_h, ed),
            (pn, pn_v),
            (pb, pb_v),
            (mn, mn_v),
            (mb, mb_v),
            (en, en_v),
            (eb, eb_v),
        ))
    ]

    pl.semaphore_wait(barrier, n)

    send_u, send_d = [], []
    for at in range(chunks):
        span = pl.ds(at * part_u, part_u)
        send_u.append(pltpu.make_async_remote_copy(
            src_ref=pu.at[pl.ds(pl.multiple_of(peer * rows + at * part_u, 8), part_u), :],
            dst_ref=got_u.at[span, :],
            send_sem=part_send.at[0, at],
            recv_sem=part_recv.at[0, at],
            device_id={"dp": peer},
        ))
        span = pl.ds(at * part_d, part_d)
        send_d.append(pltpu.make_async_remote_copy(
            src_ref=pd.at[span, theirs(cols)],
            dst_ref=got_d.at[span, :],
            send_sem=part_send.at[1, at],
            recv_sem=part_recv.at[1, at],
            device_id={"dp": peer},
        ))
    for load, copy in zip(give[:chunks], send_u):
        copy.start()
    for load in (loads[0], loads[2], *loads[6:]):
        load.start()
    for load, copy in zip(give[chunks:], send_d):
        copy.start()
    for load in (loads[1], *loads[3:6]):
        load.start()

    half = mn.shape[-1]
    for load in loads[6:]:
        load.wait()
    vec[0:1, :] = pn_v[...]
    vec[1:2, :] = pb_v[...]
    vec[2:3, :half] = mn_v[...].reshape(1, half)
    vec[2:3, half:] = en_v[...].reshape(1, half)
    vec[3:4, :half] = mb_v[...].reshape(1, half)
    vec[3:4, half:] = eb_v[...].reshape(1, half)

    step_u, step_d = 32, 64

    loads[0].wait()

    @pl.loop(0, rows // step_u)
    def _(at):
        span = pl.ds(pl.multiple_of(at * step_u, step_u), step_u)
        x = mu[span, :]
        sq_u[span, :] = lane_sums(x * x)

    stat_u[pl.ds(here, 1), 0:1, :] = jnp.sum(sq_u[...].T, axis=0).reshape(1, 1, rows)

    def down_squares(read, start, count):
        @pl.loop(0, count // step_d)
        def _(at):
            span = pl.ds(pl.multiple_of(start + at * step_d, step_d), step_d)
            x = read(span)
            acc_d[...] += jnp.sum((x * x).reshape(step_d // 8, 8, cols), axis=0)

    send_vec = pltpu.make_async_remote_copy(
        src_ref=vec, dst_ref=got_vec, send_sem=vec_sem.at[0], recv_sem=vec_sem.at[1],
        device_id={"dp": peer},
    )
    send_vec.start()

    loads[1].wait()
    acc_d[...] = jnp.zeros_like(acc_d)
    down_squares(lambda span: md[span, :], 0, tall)
    stat_d[pl.ds(here, 1), 0:1, :] = jnp.sum(acc_d[...], axis=0).reshape(1, 1, cols)
    acc_d[...] = jnp.zeros_like(acc_d)

    def to_peers(stat, which):
        copies = []
        for step in range(1, n):
            copies.append(pltpu.make_async_remote_copy(
                src_ref=stat.at[here],
                dst_ref=stat.at[here],
                send_sem=stat_send.at[which, step - 1],
                recv_sem=stat_recv.at[which, step - 1],
                device_id={"tp": lax.rem(here + step, n)},
            ))
        for copy in copies:
            copy.start()
        return copies

    loads[2].wait()
    for chunk in range(chunks):
        send_u[chunk].wait_recv()

        @pl.loop(0, part_u // step_u)
        def _(at):
            span = pl.ds(pl.multiple_of(chunk * part_u + at * step_u, step_u), step_u)
            x = (own_u[span, :] + got_u[span, :]) * rate
            own_u[span, :] = x
            sq_u[span, :] = lane_sums(x * x)

    stat_u[pl.ds(here, 1), 1:2, :] = jnp.sum(sq_u[...].T, axis=0).reshape(1, 1, rows)
    stats_u = to_peers(stat_u, 0)

    loads[3].wait()

    def summed(span):
        x = (own_d[span, :] + got_d[span, :]) * rate
        own_d[span, :] = x
        return x

    for chunk in range(chunks):
        send_d[chunk].wait_recv()
        down_squares(summed, chunk * part_d, part_d)
    stat_d[pl.ds(here, 1), 1:2, :] = jnp.sum(acc_d[...], axis=0).reshape(1, 1, cols)
    stats_d = to_peers(stat_d, 1)

    send_vec.wait()
    mean = (vec[0:2, :] + got_vec[0:2, :]) * rate
    for at, (state, stepped, rounded) in enumerate(((tn, sn, cn), (tb, sb, cb))):
        row = slice(2 + at, 3 + at)
        low, high = mean[at : at + 1, :half], mean[at : at + 1, half:]
        new_own = hold_rate * vec[row, half:] + jnp.where(me == 0, low, high)
        own = vec[row, :half] - learn_rate * new_own
        new_other = hold_rate * got_vec[row, half:] + jnp.where(me == 0, high, low)
        other = got_vec[row, :half] - learn_rate * new_other
        state[...] = new_own.reshape(state.shape)
        stepped[...] = own.reshape(stepped.shape)
        whole = jnp.concatenate(
            [jnp.where(me == 0, own, other), jnp.where(me == 0, other, own)], axis=1
        )
        rounded[...] = whole.reshape(rounded.shape).astype(rounded.dtype)

    def ratio_of(stat):
        total = stat[0]
        for at in range(1, n):
            total = total + stat[at]
        return jnp.sqrt(total[0:1, :]) * lax.rsqrt(total[1:2, :] + 1e-06)

    loads[4].wait()
    for copy in stats_u:
        copy.wait()
    sq_u[...] = jnp.broadcast_to(ratio_of(stat_u), (lanes, rows)).T

    out = []
    for piece in range(pieces):
        size = rows // pieces

        @pl.loop(0, size // step_u)
        def _(at):
            start = piece * size + at * step_u
            span = pl.ds(pl.multiple_of(start, step_u), step_u)
            ratio = sq_u[span, :]
            ratio = jnp.concatenate([ratio] * (wide // lanes), axis=1)
            state = hold_rate * eu[span, :] + own_u[span, :] * ratio
            stepped = mu[span, :] - learn_rate * state
            tu[span, :] = state
            su[span, :] = stepped
            place = pl.ds(pl.multiple_of(me * rows + start, step_u), step_u)
            cu[place, :] = stepped.astype(cu.dtype)

        span = pl.ds(pl.multiple_of(me * rows + piece * size, step_u), size)
        out.append(pltpu.make_async_remote_copy(
            src_ref=cu.at[span, :],
            dst_ref=cu.at[span, :],
            send_sem=out_send.at[0, piece],
            recv_sem=out_recv.at[0, piece],
            device_id={"dp": peer},
        ))
        out[-1].start()

    loads[5].wait()
    for copy in stats_d:
        copy.wait()
    ratio_d = ratio_of(stat_d)
    acc_d[...] = jnp.broadcast_to(ratio_d, acc_d.shape)
    for piece in range(pieces):
        size = tall // pieces

        @pl.loop(0, size // step_d)
        def _(at):
            span = pl.ds(pl.multiple_of(piece * size + at * step_d, step_d), step_d)
            ratio = jnp.broadcast_to(acc_d[...][None], (step_d // 8, 8, cols)).reshape(step_d, cols)
            state = hold_rate * ed[span, :] + own_d[span, :] * ratio
            stepped = md[span, :] - learn_rate * state
            td[span, :] = state
            sd[span, :] = stepped
            cd[span, mine(cols)] = stepped.astype(cd.dtype)

        span = pl.ds(piece * size, size)
        out.append(pltpu.make_async_remote_copy(
            src_ref=cd.at[span, mine(cols)],
            dst_ref=cd.at[span, mine(cols)],
            send_sem=out_send.at[1, piece],
            recv_sem=out_recv.at[1, piece],
            device_id={"dp": peer},
        ))
        out[-1].start()

    for copy in send_u + send_d:
        copy.wait_send()
    for copy in out:
        copy.wait()


def place_results(*refs):
    count = (len(refs) - 1) // 2
    sem = refs[-1]
    copies = [
        pltpu.make_async_copy(refs[at], refs[count + at], sem.at[at]) for at in range(count)
    ]
    for copy in copies:
        copy.start()
    for copy in copies:
        copy.wait()


def held(arrays):
    return [pltpu.with_memory_space_constraint(x, pltpu.HBM) for x in arrays]


def on_pair(*args):
    pu, pd, pn, pb, mu, md, mn, mb, eu, ed, en, eb = args
    n = lax.axis_size("tp")
    f32, bf16 = jnp.float32, jnp.bfloat16
    vmem = pl.BlockSpec(memory_space=pltpu.VMEM)
    hbm = pl.BlockSpec(memory_space=pltpu.HBM)
    wide, tall = pu.shape[2], pd.shape[1]
    outs = (
        ((pu.shape[1], wide), bf16),
        ((tall, pd.shape[2]), bf16),
        ((pn.shape[1],), bf16),
        ((pb.shape[1],), bf16),
        *((x.shape, f32) for x in (mu, md, mn, mb)),
        *((x.shape, f32) for x in (mu, md, mn, mb)),
    )
    rows, cols = mu.shape[0], md.shape[1]
    results = pl.pallas_call(
        exchange,
        out_shape=[jax.ShapeDtypeStruct(shape, dtype) for shape, dtype in outs],
        in_specs=[hbm] * len(args),
        out_specs=[vmem] * len(outs),
        scratch_shapes=[
            *(pltpu.VMEM(x.shape, f32) for x in (mu, md) * 5),
            *(pltpu.VMEM(x.shape, f32) for x in (pn, pb, mn, mb, en, eb)),
            pltpu.VMEM((4, pn.shape[1]), f32),
            pltpu.VMEM((4, pn.shape[1]), f32),
            pltpu.VMEM((rows, lanes), f32),
            pltpu.VMEM((8, cols), f32),
            pltpu.VMEM((n, 2, rows), f32),
            pltpu.VMEM((n, 2, cols), f32),
            pltpu.SemaphoreType.DMA((12,)),
            pltpu.SemaphoreType.DMA((2, chunks)),
            pltpu.SemaphoreType.DMA((2, chunks)),
            pltpu.SemaphoreType.DMA((2, chunks)),
            pltpu.SemaphoreType.DMA((2,)),
            pltpu.SemaphoreType.DMA((2, n - 1)),
            pltpu.SemaphoreType.DMA((2, n - 1)),
            pltpu.SemaphoreType.DMA((2, pieces)),
            pltpu.SemaphoreType.DMA((2, pieces)),
        ],
        compiler_params=pltpu.CompilerParams(
            collective_id=0, has_side_effects=True, vmem_limit_bytes=40 * 2**20
        ),
        name="exchange",
    )(*held((pu[0], pd[0], *args[2:])))
    return tuple(pl.pallas_call(
        place_results,
        out_shape=[jax.ShapeDtypeStruct(shape, dtype) for shape, dtype in outs],
        in_specs=[vmem] * len(outs),
        out_specs=[hbm] * len(outs),
        scratch_shapes=[pltpu.SemaphoreType.DMA((len(outs),))],
        compiler_params=pltpu.CompilerParams(vmem_limit_bytes=2**20),
        name="place_results",
    )(*results))


def solution(mesh):
    in_specs = (
        P(("job", "dp"), None, "tp"),
        P(("job", "dp"), "tp", None),
        P(("job", "dp"), None),
        P(("job", "dp"), None),
        P(("job", "dp"), "tp"),
        P(("job", "tp"), "dp"),
        P(("job", "dp")),
        P(("job", "dp")),
        P(("job", "dp"), "tp"),
        P(("job", "tp"), "dp"),
        P(("job", "dp")),
        P(("job", "dp")),
    )
    out_specs = (
        P("job", "tp"),
        P(("job", "tp"), None),
        P("job"),
        P("job"),
        P(("job", "dp"), "tp"),
        P(("job", "tp"), "dp"),
        P(("job", "dp")),
        P(("job", "dp")),
        P(("job", "dp"), "tp"),
        P(("job", "tp"), "dp"),
        P(("job", "dp")),
        P(("job", "dp")),
    )
    return jax.shard_map(
        on_device if mesh.shape["dp"] != 2 else on_pair, mesh=mesh, in_specs=in_specs, out_specs=out_specs, check_vma=False
    )
```

profile of v0, /device:TPU:0, one launch (start us, length us, event | category | flops | bytes accessed | tf_op | source)
XLA Modules:
  0.0 17.6 jit_solution(3983953278076039597)
XLA Ops:
  0.6 13.8 %exchange.1 = (bf16[768,768]{1,0:T(8,128)(2,1)S(1)}, bf16[768,768]{1,0:T(8,128)(2,1)S(1)}, bf16[768]{0:T(1024)(128)(2,1)S(1)}, bf16[768]{0:T(1024)(128)(2,1)S(1)...) custom-call(f32[768,768]{1,0:T(8,128)} %bitcast.2, ...), custom_call_target="tpu_custom_call" | custom-call | tf_op jit(solution)/shard_map/exchange/pallas_call | solution.py:387
  14.5 3.1 %place_results.1 = (bf16[768,768]{1,0:T(8,128)(2,1)}, bf16[768,768]{1,0:T(8,128)(2,1)}, bf16[768]{0:T(1024)(128)(2,1)}, bf16[768]{0:T(1024)(128)(2,1)}, f32[384,...) custom-call(bf16[768,768]{1,0:T(8,128)(2,1)S(1)} %get-tuple-element., ...), custom_call_target="tpu_custom_call" | custom-call | tf_op jit(solution)/shard_map/place_results/pallas_call | solution.py:416
where the time goes:
time: 17.7 us; the launch traced here: 17.6 us
  Pallas kernels  16.9 us (95%)
  between operations  0.66 us (4%)
    pallas_call x1, Pallas kernels, on_pair(): pl.pallas_call(exchange, out_shape=[jax.ShapeDtypeStruct(shape, dtype) fo...  13.8 us
    pallas_call x1, Pallas kernels, on_pair(): pl.pallas_call(place_results, out_shape=[jax.ShapeDtypeStruct(shape, dtyp...  3.06 us

commit v1 on v0

v1 whole, which is shorter than its diff:
```python
import functools

import jax
import jax.numpy as jnp
from jax import lax
from jax.experimental import pallas as pl
from jax.experimental.pallas import tpu as pltpu
from jax.sharding import PartitionSpec as P

learn_rate = 0.4
hold_rate = 0.9


def on_device(
    partial_up,
    partial_down,
    partial_norm,
    partial_bias,
    master_up,
    master_down,
    master_norm,
    master_bias,
    memory_up,
    memory_down,
    memory_norm,
    memory_bias,
):
    mean_up, mean_down = (
        lax.psum_scatter(partial_up[0], "dp", scatter_dimension=0, tiled=True),
        lax.psum_scatter(partial_down[0], "dp", scatter_dimension=1, tiled=True),
    )
    whole_norm, whole_bias = lax.psum((partial_norm[0], partial_bias[0]), "dp")
    place = lax.axis_index("dp")
    mean_norm = lax.dynamic_slice_in_dim(
        whole_norm, place * master_norm.shape[0], master_norm.shape[0]
    )
    mean_bias = lax.dynamic_slice_in_dim(
        whole_bias, place * master_bias.shape[0], master_bias.shape[0]
    )
    mean_rate = lax.axis_size("dp") ** (-0.5)
    mean_up = mean_up * mean_rate
    mean_down = mean_down * mean_rate
    mean_norm = mean_norm * mean_rate
    mean_bias = mean_bias * mean_rate
    own_up, own_down, slope_up_norm, slope_down_norm = lax.psum(
        (
            jnp.sum(master_up * master_up, axis=1, keepdims=True),
            jnp.sum(master_down * master_down, axis=0, keepdims=True),
            jnp.sum(mean_up * mean_up, axis=1, keepdims=True),
            jnp.sum(mean_down * mean_down, axis=0, keepdims=True),
        ),
        "tp",
    )
    mean_up = mean_up * (jnp.sqrt(own_up) * lax.rsqrt(slope_up_norm + 1e-06))
    mean_down = mean_down * (jnp.sqrt(own_down) * lax.rsqrt(slope_down_norm + 1e-06))
    state_new_up = hold_rate * memory_up + mean_up
    stepped_up = master_up - learn_rate * state_new_up
    state_new_down = hold_rate * memory_down + mean_down
    stepped_down = master_down - learn_rate * state_new_down
    state_new_norm = hold_rate * memory_norm + mean_norm
    stepped_norm = master_norm - learn_rate * state_new_norm
    state_new_bias = hold_rate * memory_bias + mean_bias
    stepped_bias = master_bias - learn_rate * state_new_bias
    compute_up, compute_down, compute_norm, compute_bias = (
        lax.all_gather(stepped_up.astype(jnp.bfloat16), "dp", axis=0, tiled=True),
        lax.all_gather(stepped_down.astype(jnp.bfloat16), "dp", axis=1, tiled=True),
        lax.all_gather(stepped_norm.astype(jnp.bfloat16), "dp", axis=0, tiled=True),
        lax.all_gather(stepped_bias.astype(jnp.bfloat16), "dp", axis=0, tiled=True),
    )
    return (
        compute_up,
        compute_down,
        compute_norm,
        compute_bias,
        stepped_up,
        stepped_down,
        stepped_norm,
        stepped_bias,
        state_new_up,
        state_new_down,
        state_new_norm,
        state_new_bias,
    )


chunks = 4
pieces = 4
lanes = 128
gathered = 2


def lane_sums(x):
    total = x[:, :lanes]
    for at in range(lanes, x.shape[1], lanes):
        total = total + x[:, at : at + lanes]
    return total


def blocks(count, step):
    def over(body):
        @pl.loop(0, count // step)
        def _(at):
            body(pl.multiple_of(at * step, step))

    return over


def wait_for(ref, sem):
    pltpu.make_async_copy(ref, ref, sem).wait()


def scale_of(total, rate):
    return jnp.sqrt(total[0:1, :]) * (lax.rsqrt(total[1:2, :] * (rate * rate) + 1e-06) * rate)


def scale_at(stat, first, n, rate):
    total = stat[first]
    for at in range(1, n):
        total = total + stat[first + at]
    return scale_of(total, rate)


def exchange(
    pu, pd, pn, pb, mu_h, md_h, mn, mb, eu_h, ed_h, en, eb,
    cu, cn, cb, su, sn, sb, tu, tn, tb,
    sum_d, base_d, ed, give_d, other_d, stat_d,
    own_u, own_d, give_u, sum_u, base_u, other_u, mu, md, eu,
    pn_v, pb_v, mn_v, mb_v, en_v, eb_v, vec, got_vec,
    sq_u, sq_o, acc_d, stat_u, stat_w,
    load_sem, small_sem, part_sem, send_sem, stat_sem, more_sem, hello, ready,
):
    me = lax.axis_index("dp")
    peer = 1 - me
    here = lax.axis_index("tp")
    n = lax.axis_size("tp")
    rate = lax.axis_size("dp") ** (-0.5)
    rows, wide = mu.shape
    tall, cols = md.shape
    groups = rows // lanes
    part_d = tall // chunks
    step_u, step_d = 32, 64
    first = gathered * lanes
    rest = pl.ds(first, rows - first)

    def at_core(core, size, start=0, count=None):
        return pl.ds(pl.multiple_of(core * size + start, 8), size if count is None else count)

    def columns(core):
        return pl.ds(pl.multiple_of(core * cols, cols), cols)

    def load(source, target, sem):
        copy = pltpu.make_async_copy(source, target, sem)
        copy.start()
        return copy

    small = [
        load(source, target, small_sem.at[at])
        for at, (source, target) in enumerate(
            ((pn, pn_v), (pb, pb_v), (mn, mn_v), (mb, mb_v), (en, en_v), (eb, eb_v))
        )
    ]
    load(pu.at[at_core(me, rows), :], own_u, load_sem.at[1])
    load(mu_h, mu, load_sem.at[0])

    barrier = pltpu.get_barrier_semaphore()

    @pl.when(me == 1)
    def _():
        pl.semaphore_signal(barrier, inc=1, device_id={"dp": peer})

    @pl.when(me == 0)
    def _():
        pl.semaphore_wait(barrier, 1)
        pl.semaphore_signal(hello, inc=1, device_id={"dp": peer})

    @pl.when(me == 1)
    def _():
        pl.semaphore_wait(hello, 1)
        for step in range(1, n):
            pl.semaphore_signal(barrier, inc=1, device_id={"tp": lax.rem(here + step, n)})

    def to_peer(source, target, send, recv):
        copy = pltpu.make_async_remote_copy(
            src_ref=source, dst_ref=target, send_sem=send_sem.at[send], recv_sem=recv, device_id={"dp": peer}
        )
        copy.start()
        return copy

    spans_u = [pl.ds(at * lanes, lanes) for at in range(groups)]
    spans_d = [pl.ds(0, tall - part_d), pl.ds(tall - part_d, part_d)]
    sent = [
        to_peer(pu.at[at_core(peer, rows, at * lanes, lanes), :], sum_u.at[span, :], 0, part_sem.at[at])
        for at, span in enumerate(spans_u)
    ] + [
        to_peer(pd.at[span, columns(peer)], sum_d.at[span, :], 0, part_sem.at[groups + at])
        for at, span in enumerate(spans_d)
    ]
    load(md_h, md, load_sem.at[2])
    load(ed_h, ed, load_sem.at[3])
    load(eu_h, eu, load_sem.at[5])
    load(pd.at[:, columns(me)], own_d, load_sem.at[4])

    wait_for(mu, load_sem.at[0])

    @blocks(rows, step_u)
    def _(at):
        span = pl.ds(at, step_u)
        x = mu[span, :]
        sq_u[span, :] = lane_sums(x * x)

    def store_size(group, which):
        size = jnp.sum(sq_u[spans_u[group], :].T, axis=0).reshape(1, 1, lanes)
        if group < gathered:
            stat_u[pl.ds(group * n + here, 1), which : which + 1, :] = size
        else:
            at = (2 * (group - gathered) + me) * n + here
            stat_w[pl.ds(at, 1), which : which + 1, :] = size

    for group in range(groups):
        store_size(group, 0)

    def sizes(ref, at, send, recv, cores):
        for step in range(n):
            for core in range(cores):
                if step + core > 0:
                    pltpu.make_async_remote_copy(
                        src_ref=ref.at[at],
                        dst_ref=ref.at[at],
                        send_sem=send_sem.at[send],
                        recv_sem=recv,
                        device_id={"dp": peer if core else me, "tp": lax.rem(here + step, n)},
                    ).start()

    wait_for(own_u, load_sem.at[1])
    load(pu.at[at_core(peer, rows, first, rows - first), :], give_u, load_sem.at[6])
    load(pd.at[:, columns(peer)], give_d, load_sem.at[7])
    def sum_rows(group):
        sent[group].wait_recv()

        @blocks(lanes, step_u)
        def _(at):
            span = pl.ds(pl.multiple_of(group * lanes + at, step_u), step_u)
            x = own_u[span, :] + sum_u[span, :]
            sum_u[span, :] = x
            sq_u[span, :] = lane_sums(x * x)

        store_size(group, 1)

    def send_sizes(group):
        if group < gathered:
            sizes(stat_u, group * n + here, 1, stat_sem.at[group], 1)
        else:
            sizes(stat_w, (2 * (group - gathered) + me) * n + here, 2, stat_sem.at[group], 2)

    sum_rows(0)
    half = mn.shape[-1]
    for copy in small:
        copy.wait()
    vec[0:1, :] = pn_v[...]
    vec[1:2, :] = pb_v[...]
    vec[2:3, :half] = mn_v[...].reshape(1, half)
    vec[2:3, half:] = en_v[...].reshape(1, half)
    vec[3:4, :half] = mb_v[...].reshape(1, half)
    vec[3:4, half:] = eb_v[...].reshape(1, half)
    send_vec = to_peer(vec, got_vec, 6, more_sem.at[2])

    wait_for(md, load_sem.at[2])
    wait_for(ed, load_sem.at[3])
    acc_d[...] = jnp.zeros_like(acc_d)

    def eighths(x):
        return jnp.sum(x.reshape(step_d // 8, 8, cols), axis=0)

    @blocks(tall, step_d)
    def _(at):
        span = pl.ds(at, step_d)
        x = md[span, :]
        base_d[span, :] = x - (learn_rate * hold_rate) * ed[span, :]
        acc_d[...] += eighths(x * x)

    slot_d = me * n + here
    stat_d[pl.ds(slot_d, 1), 0:1, :] = jnp.sum(acc_d[...], axis=0).reshape(1, 1, cols)
    acc_d[...] = jnp.zeros_like(acc_d)
    wait_for(eu, load_sem.at[5])

    @blocks(rows - first, step_u)
    def _(at):
        span = pl.ds(pl.multiple_of(first + at, step_u), step_u)
        base_u[pl.ds(at, step_u), :] = mu[span, :] - (learn_rate * hold_rate) * eu[span, :]

    wait_for(own_d, load_sem.at[4])
    to_peer(own_u.at[rest, :], other_u.at[0], 3, more_sem.at[0])
    to_peer(base_u, other_u.at[1], 3, more_sem.at[0])
    to_peer(own_d, other_d.at[0], 4, more_sem.at[1])
    to_peer(base_d, other_d.at[1], 4, more_sem.at[1])

    for group in range(1, groups - 1):
        sum_rows(group)
    @pl.when(me == 1)
    def _():
        pl.semaphore_wait(barrier, n - 1)
        pl.semaphore_signal(ready, inc=1, device_id={"dp": peer})

    @pl.when(me == 0)
    def _():
        pl.semaphore_wait(ready, 1)

    for group in range(groups - 1):
        send_sizes(group)
    sum_rows(groups - 1)
    send_sizes(groups - 1)

    for chunk, part in enumerate(spans_d):
        sent[groups + chunk].wait_recv()

        @blocks(part.size, step_d)
        def _(at):
            span = pl.ds(pl.multiple_of(part.start + at, step_d), step_d)
            x = own_d[span, :] + sum_d[span, :]
            sum_d[span, :] = x
            acc_d[...] += eighths(x * x)

    stat_d[pl.ds(slot_d, 1), 1:2, :] = jnp.sum(acc_d[...], axis=0).reshape(1, 1, cols)
    sizes(stat_d, slot_d, 5, stat_sem.at[groups], 2)

    for group in range(groups):
        span = spans_u[group]
        if group < gathered:
            wait_for(stat_u.at[pl.ds(0, n - 1)], stat_sem.at[group])
            sq_u[span, :] = jnp.broadcast_to(scale_at(stat_u, group * n, n, rate), (lanes, lanes)).T
        else:
            wait_for(stat_w.at[pl.ds(0, 2 * n - 1)], stat_sem.at[group])
            at = 2 * (group - gathered)
            sq_u[span, :] = jnp.broadcast_to(scale_at(stat_w, (at + me) * n, n, rate), (lanes, lanes)).T
            sq_o[pl.ds((group - gathered) * lanes, lanes), :] = jnp.broadcast_to(
                scale_at(stat_w, (at + peer) * n, n, rate), (lanes, lanes)
            ).T
        if group < gathered:

            @blocks(lanes, step_u)
            def _(at):
                start = pl.multiple_of(group * lanes + at, step_u)
                span = pl.ds(start, step_u)
                scale = jnp.concatenate([sq_u[span, :]] * (wide // lanes), axis=1)
                state = hold_rate * eu[span, :] + sum_u[span, :] * scale
                stepped = mu[span, :] - learn_rate * state
                tu[span, :] = state
                su[span, :] = stepped
                cu[pl.ds(pl.multiple_of(me * rows + start, step_u), step_u), :] = stepped.astype(cu.dtype)

            part = cu.at[at_core(me, rows, group * lanes, lanes), :]
            to_peer(part, part, 7, more_sem.at[3])
        else:
            if group == gathered:
                wait_for(other_u, more_sem.at[0])
                wait_for(give_u, load_sem.at[6])

            @blocks(lanes, step_u // 2)
            def _(at):
                inner = pl.multiple_of((group - gathered) * lanes + at, step_u // 2)
                start = pl.multiple_of(group * lanes + at, step_u // 2)
                near, span = pl.ds(inner, step_u // 2), pl.ds(start, step_u // 2)
                scale = jnp.concatenate([sq_u[span, :]] * (wide // lanes), axis=1)
                step = sum_u[span, :] * scale
                tu[span, :] = hold_rate * eu[span, :] + step
                stepped = base_u[near, :] - learn_rate * step
                su[span, :] = stepped
                place = pl.ds(pl.multiple_of(me * rows + start, step_u // 2), step_u // 2)
                cu[place, :] = stepped.astype(cu.dtype)
                scale = jnp.concatenate([sq_o[near, :]] * (wide // lanes), axis=1)
                step = (give_u[near, :] + other_u[0, near, :]) * scale
                stepped = other_u[1, near, :] - learn_rate * step
                place = pl.ds(pl.multiple_of(peer * rows + start, step_u // 2), step_u // 2)
                cu[place, :] = stepped.astype(cu.dtype)

    send_vec.wait_recv()
    mean = (vec[0:2, :] + got_vec[0:2, :]) * rate
    for at, (state, stepped, rounded) in enumerate(((tn, sn, cn), (tb, sb, cb))):
        row = slice(2 + at, 3 + at)
        low, high = mean[at : at + 1, :half], mean[at : at + 1, half:]
        new_own = hold_rate * vec[row, half:] + jnp.where(me == 0, low, high)
        own = vec[row, :half] - learn_rate * new_own
        new_other = hold_rate * got_vec[row, half:] + jnp.where(me == 0, high, low)
        other = got_vec[row, :half] - learn_rate * new_other
        state[...] = new_own.reshape(state.shape)
        stepped[...] = own.reshape(stepped.shape)
        whole = jnp.concatenate(
            [jnp.where(me == 0, own, other), jnp.where(me == 0, other, own)], axis=1
        )
        rounded[...] = whole.reshape(rounded.shape).astype(rounded.dtype)

    wait_for(give_d, load_sem.at[7])
    wait_for(other_d, more_sem.at[1])
    wait_for(other_d, send_sem.at[0])
    wait_for(other_u, send_sem.at[3])
    wait_for(other_d, send_sem.at[4])
    send_vec.wait_send()
    wait_for(stat_u.at[pl.ds(0, gathered * (n - 1))], send_sem.at[1])
    wait_for(stat_w.at[pl.ds(0, (groups - gathered) * (2 * n - 1))], send_sem.at[2])
    wait_for(stat_d.at[pl.ds(0, 2 * n - 1)], stat_sem.at[groups])
    wait_for(stat_d.at[pl.ds(0, 2 * n - 1)], send_sem.at[5])
    wait_for(cu.at[at_core(peer, rows, 0, first), :], more_sem.at[3])
    wait_for(cu.at[at_core(me, rows, 0, first), :], send_sem.at[7])


def finish(
    cu_v, cn_v, cb_v, su_v, sn_v, sb_v, tu_v, tn_v, tb_v,
    sum_d, base_d, ed, give_d, other_d, stat_d,
    cu, cd, cn, cb, su, sd, sn, sb, tu, td, tn, tb,
    cd_v, sd_v, td_v, sem,
):
    me = lax.axis_index("dp")
    rate = lax.axis_size("dp") ** (-0.5)
    n = lax.axis_size("tp")
    tall, cols = td_v.shape
    step = 32

    def out(source, target, at):
        copy = pltpu.make_async_copy(source, target, sem.at[at])
        copy.start()
        return copy

    small = [
        out(source, target, 4 + at)
        for at, (source, target) in enumerate(
            ((cn_v, cn), (cb_v, cb), (sn_v, sn), (sb_v, sb), (tn_v, tn), (tb_v, tb))
        )
    ]
    out(su_v, su, 0)
    out(tu_v, tu, 0)
    out(cu_v, cu, 1)

    own, other = (scale_at(stat_d, core * n, n, rate) for core in (me, 1 - me))
    for piece in range(pieces):
        size = tall // pieces

        @blocks(size, step)
        def _(at):
            span = pl.ds(pl.multiple_of(piece * size + at, step), step)
            x = sum_d[span, :] * own
            td_v[span, :] = hold_rate * ed[span, :] + x
            stepped = base_d[span, :] - learn_rate * x
            sd_v[span, :] = stepped
            cd_v[span, pl.ds(pl.multiple_of(me * cols, cols), cols)] = stepped.astype(cd_v.dtype)
            x = (give_d[span, :] + other_d[0, span, :]) * other
            stepped = other_d[1, span, :] - learn_rate * x
            cd_v[span, pl.ds(pl.multiple_of((1 - me) * cols, cols), cols)] = stepped.astype(cd_v.dtype)

        span = pl.ds(piece * size, size)
        out(td_v.at[span, :], td.at[span, :], 2)
        out(sd_v.at[span, :], sd.at[span, :], 2)
        out(cd_v.at[span, :], cd.at[span, :], 3)
    for copy in small:
        copy.wait()
    wait_for(other_d, sem.at[0])
    wait_for(cu_v, sem.at[1])
    wait_for(other_d, sem.at[2])
    wait_for(cd_v, sem.at[3])


def held(arrays):
    return [pltpu.with_memory_space_constraint(x, pltpu.HBM) for x in arrays]


def on_pair(*args):
    pu, pd, pn, pb, mu, md, mn, mb, eu, ed, en, eb = args
    n = lax.axis_size("tp")
    f32, bf16 = jnp.float32, jnp.bfloat16
    vmem = pl.BlockSpec(memory_space=pltpu.VMEM)
    hbm = pl.BlockSpec(memory_space=pltpu.HBM)
    wide, tall = pu.shape[2], pd.shape[1]
    rows, cols = mu.shape[0], md.shape[1]
    groups = rows // lanes
    rest = rows - gathered * lanes
    dma = pltpu.SemaphoreType.DMA

    def shaped(shape, dtype=f32):
        return jax.ShapeDtypeStruct(shape, dtype)

    between = [
        shaped((pu.shape[1], wide), bf16), shaped((pn.shape[1],), bf16), shaped((pb.shape[1],), bf16),
        *(shaped(x.shape) for x in (mu, mn, mb)),
        *(shaped(x.shape) for x in (mu, mn, mb)),
        *(shaped(md.shape) for _ in range(4)),
        shaped((2, *md.shape)),
        shaped((2 * n, 2, cols)),
    ]
    results = pl.pallas_call(
        exchange,
        out_shape=between,
        in_specs=[hbm] * len(args),
        out_specs=[vmem] * len(between),
        scratch_shapes=[
            pltpu.VMEM(mu.shape, f32),
            pltpu.VMEM(md.shape, f32),
            pltpu.VMEM((rest, wide), f32),
            pltpu.VMEM(mu.shape, f32),
            pltpu.VMEM((rest, wide), f32),
            pltpu.VMEM((2, rest, wide), f32),
            *(pltpu.VMEM(x.shape, f32) for x in (mu, md, mu)),
            *(pltpu.VMEM(x.shape, f32) for x in (pn, pb, mn, mb, en, eb)),
            pltpu.VMEM((4, pn.shape[1]), f32),
            pltpu.VMEM((4, pn.shape[1]), f32),
            pltpu.VMEM((rows, lanes), f32),
            pltpu.VMEM((rest, lanes), f32),
            pltpu.VMEM((8, cols), f32),
            pltpu.VMEM((gathered * n, 2, lanes), f32),
            pltpu.VMEM(((groups - gathered) * 2 * n, 2, lanes), f32),
            dma((8,)),
            dma((6,)),
            dma((groups + 2,)),
            dma((8,)),
            dma((groups + 1,)),
            dma((4,)),
            pltpu.SemaphoreType.REGULAR,
            pltpu.SemaphoreType.REGULAR,
        ],
        compiler_params=pltpu.CompilerParams(
            collective_id=0, has_side_effects=True, vmem_limit_bytes=40 * 2**20
        ),
        name="exchange",
    )(*held((pu[0], pd[0], *args[2:])))
    outs = (
        ((pu.shape[1], wide), bf16),
        ((tall, pd.shape[2]), bf16),
        ((pn.shape[1],), bf16),
        ((pb.shape[1],), bf16),
        *((x.shape, f32) for x in (mu, md, mn, mb)),
        *((x.shape, f32) for x in (mu, md, mn, mb)),
    )
    return tuple(pl.pallas_call(
        finish,
        out_shape=[shaped(shape, dtype) for shape, dtype in outs],
        in_specs=[vmem] * len(between),
        out_specs=[hbm] * len(outs),
        scratch_shapes=[
            pltpu.VMEM((tall, pd.shape[2]), bf16),
            pltpu.VMEM(md.shape, f32),
            pltpu.VMEM(md.shape, f32),
            dma((10,)),
        ],
        compiler_params=pltpu.CompilerParams(vmem_limit_bytes=8 * 2**20),
        name="finish",
    )(*results))


def solution(mesh):
    in_specs = (
        P(("job", "dp"), None, "tp"),
        P(("job", "dp"), "tp", None),
        P(("job", "dp"), None),
        P(("job", "dp"), None),
        P(("job", "dp"), "tp"),
        P(("job", "tp"), "dp"),
        P(("job", "dp")),
        P(("job", "dp")),
        P(("job", "dp"), "tp"),
        P(("job", "tp"), "dp"),
        P(("job", "dp")),
        P(("job", "dp")),
    )
    out_specs = (
        P("job", "tp"),
        P(("job", "tp"), None),
        P("job"),
        P("job"),
        P(("job", "dp"), "tp"),
        P(("job", "tp"), "dp"),
        P(("job", "dp")),
        P(("job", "dp")),
        P(("job", "dp"), "tp"),
        P(("job", "tp"), "dp"),
        P(("job", "dp")),
        P(("job", "dp")),
    )
    return jax.shard_map(
        on_device if mesh.shape["dp"] != 2 else on_pair, mesh=mesh, in_specs=in_specs, out_specs=out_specs, check_vma=False
    )
```

time: 17.7 us -> 15.7 us (0.89)
  Pallas kernels: 16.9 us -> 14.9 us
    pallas_call x2, Pallas kernels: 16.9 us -> 14.9 us  [the longest x1 11.9 us: on_pair(): pl.pallas_call(exchange, out_shape=between, in_specs=[hbm] * len(args), o...]
where the time goes in v1:
time: 15.7 us; the launch traced here: 15.5 us
  Pallas kernels  14.9 us (95%)
  between operations  0.66 us (4%)
    pallas_call x1, Pallas kernels, on_pair(): pl.pallas_call(exchange, out_shape=between, in_specs=[hbm] * len(args), o...  11.9 us
    pallas_call x1, Pallas kernels, on_pair(): pl.pallas_call(finish, out_shape=[shaped(shape, dtype) for shape, dtype i...  3 us

profile of v1, /device:TPU:0, one launch (start us, length us, event | category | flops | bytes accessed | tf_op | source)
XLA Modules:
  0.0 15.5 jit_solution(14078678757293182711)
XLA Ops:
  0.6 11.9 %exchange.1 = (bf16[768,768]{1,0:T(8,128)(2,1)S(1)}, bf16[768]{0:T(1024)(128)(2,1)S(1)}, bf16[768]{0:T(1024)(128)(2,1)S(1)}, f32[384,768]{1,0:T(8,128)S(1)}, f32...) custom-call(f32[768,768]{1,0:T(8,128)} %bitcast.2, ...), custom_call_target="tpu_custom_call" | custom-call | tf_op jit(solution)/shard_map/exchange/pallas_call | solution.py:488
  12.5 3.0 %finish.1 = (bf16[768,768]{1,0:T(8,128)(2,1)}, bf16[768,768]{1,0:T(8,128)(2,1)}, bf16[768]{0:T(1024)(128)(2,1)}, bf16[768]{0:T(1024)(128)(2,1)}, f32[384,768]{1,...) custom-call(bf16[768,768]{1,0:T(8,128)(2,1)S(1)} %get-tuple-element., ...), custom_call_target="tpu_custom_call" | custom-call | tf_op jit(solution)/shard_map/finish/pallas_call | solution.py:531

commit v2 on v1

--- a/solution.py
+++ b/solution.py
@@ -83,7 +83,6 @@
     )
 
 
-chunks = 4
 pieces = 4
 lanes = 128
 gathered = 2
@@ -109,24 +108,24 @@
     pltpu.make_async_copy(ref, ref, sem).wait()
 
 
-def scale_of(total, rate):
-    return jnp.sqrt(total[0:1, :]) * (lax.rsqrt(total[1:2, :] * (rate * rate) + 1e-06) * rate)
+def scale_of(weights, sizes, rate):
+    return jnp.sqrt(weights) * (lax.rsqrt(sizes * (rate * rate) + 1e-06) * rate)
 
 
 def scale_at(stat, first, n, rate):
     total = stat[first]
     for at in range(1, n):
         total = total + stat[first + at]
-    return scale_of(total, rate)
+    return scale_of(total[0:1, :], total[1:2, :], rate)
 
 
 def exchange(
     pu, pd, pn, pb, mu_h, md_h, mn, mb, eu_h, ed_h, en, eb,
     cu, cn, cb, su, sn, sb, tu, tn, tb,
-    sum_d, base_d, ed, give_d, other_d, stat_d,
+    pack, ed, stat_d,
     own_u, own_d, give_u, sum_u, base_u, other_u, mu, md, eu,
     pn_v, pb_v, mn_v, mb_v, en_v, eb_v, vec, got_vec,
-    sq_u, sq_o, acc_d, stat_u, stat_w,
+    sq_u, sq_o, acc_d, acc_o, stat_u, stat_w,
     load_sem, small_sem, part_sem, send_sem, stat_sem, more_sem, hello, ready,
 ):
     me = lax.axis_index("dp")
@@ -137,8 +136,9 @@
     rows, wide = mu.shape
     tall, cols = md.shape
     groups = rows // lanes
-    part_d = tall // chunks
     step_u, step_d = 32, 64
+    shared = tall // 6 // step_d * step_d
+    other_d, (sum_d, base_d, give_d) = pack.at[pl.ds(0, 2)], (pack.at[at] for at in range(2, 5))
     first = gathered * lanes
     rest = pl.ds(first, rows - first)
 
@@ -159,7 +159,7 @@
             ((pn, pn_v), (pb, pb_v), (mn, mn_v), (mb, mb_v), (en, en_v), (eb, eb_v))
         )
     ]
-    load(pu.at[at_core(me, rows), :], own_u, load_sem.at[1])
+    load(pu.at[at_core(me, rows), :], own_u, load_sem.at[0])
     load(mu_h, mu, load_sem.at[0])
 
     barrier = pltpu.get_barrier_semaphore()
@@ -181,26 +181,36 @@
 
     def to_peer(source, target, send, recv):
         copy = pltpu.make_async_remote_copy(
-            src_ref=source, dst_ref=target, send_sem=send_sem.at[send], recv_sem=recv, device_id={"dp": peer}
+            src_ref=source, dst_ref=target, send_sem=send, recv_sem=recv, device_id={"dp": peer}
         )
         copy.start()
         return copy
 
     spans_u = [pl.ds(at * lanes, lanes) for at in range(groups)]
-    spans_d = [pl.ds(0, tall - part_d), pl.ds(tall - part_d, part_d)]
+    head, last = pl.ds(0, tall - shared), pl.ds(tall - shared, shared)
+    heads = pl.ds(0, tall - 2 * shared), pl.ds(tall - 2 * shared, shared)
     sent = [
-        to_peer(pu.at[at_core(peer, rows, at * lanes, lanes), :], sum_u.at[span, :], 0, part_sem.at[at])
+        to_peer(pu.at[at_core(peer, rows, at * lanes, lanes), :], sum_u.at[span, :], send_sem.at[0], part_sem.at[at])
         for at, span in enumerate(spans_u)
-    ] + [
-        to_peer(pd.at[span, columns(peer)], sum_d.at[span, :], 0, part_sem.at[groups + at])
-        for at, span in enumerate(spans_d)
     ]
-    load(md_h, md, load_sem.at[2])
-    load(ed_h, ed, load_sem.at[3])
-    load(eu_h, eu, load_sem.at[5])
-    load(pd.at[:, columns(me)], own_d, load_sem.at[4])
-
-    wait_for(mu, load_sem.at[0])
+    for at, span in enumerate(heads):
+        sent.append(to_peer(pd.at[span, columns(peer)], sum_d.at[span, :], send_sem.at[0], part_sem.at[groups + at]))
+
+    @pl.when(me == 0)
+    def _():
+        to_peer(pd.at[last, columns(peer)], sum_d.at[last, :], send_sem.at[0], part_sem.at[groups + 2])
+        to_peer(pd.at[last, columns(me)], other_d.at[0, last, :], send_sem.at[0], part_sem.at[groups + 3])
+
+    load(md_h, md, load_sem.at[1])
+    load(ed_h, ed, load_sem.at[1])
+    load(eu_h, eu, load_sem.at[2])
+    load(pd.at[:, columns(me)], own_d, load_sem.at[2])
+
+    wait_for(other_d, load_sem.at[0])
+    load(pd.at[:, columns(peer)], give_d, load_sem.at[0])
+    for copy in small:
+        copy.wait()
+    load(pu.at[at_core(peer, rows, first, rows - first), :], give_u, small_sem.at[0])
 
     @blocks(rows, step_u)
     def _(at):
@@ -226,14 +236,11 @@
                     pltpu.make_async_remote_copy(
                         src_ref=ref.at[at],
                         dst_ref=ref.at[at],
-                        send_sem=send_sem.at[send],
+                        send_sem=small_sem.at[send],
                         recv_sem=recv,
                         device_id={"dp": peer if core else me, "tp": lax.rem(here + step, n)},
                     ).start()
 
-    wait_for(own_u, load_sem.at[1])
-    load(pu.at[at_core(peer, rows, first, rows - first), :], give_u, load_sem.at[6])
-    load(pd.at[:, columns(peer)], give_d, load_sem.at[7])
     def sum_rows(group):
         sent[group].wait_recv()
 
@@ -252,21 +259,37 @@
         else:
             sizes(stat_w, (2 * (group - gathered) + me) * n + here, 2, stat_sem.at[group], 2)
 
-    sum_rows(0)
+    def meet():
+        @pl.when(me == 1)
+        def _():
+            pl.semaphore_wait(barrier, n - 1)
+            pl.semaphore_signal(ready, inc=1, device_id={"dp": peer})
+
+        @pl.when(me == 0)
+        def _():
+            pl.semaphore_wait(ready, 1)
+
+    for group in range(groups - 1):
+        sum_rows(group)
+
+        @pl.when(2 * here >= n)
+        def _(group=group):
+            if group == 0:
+                meet()
+            send_sizes(group)
+
     half = mn.shape[-1]
-    for copy in small:
-        copy.wait()
     vec[0:1, :] = pn_v[...]
     vec[1:2, :] = pb_v[...]
     vec[2:3, :half] = mn_v[...].reshape(1, half)
     vec[2:3, half:] = en_v[...].reshape(1, half)
     vec[3:4, :half] = mb_v[...].reshape(1, half)
     vec[3:4, half:] = eb_v[...].reshape(1, half)
-    send_vec = to_peer(vec, got_vec, 6, more_sem.at[2])
-
-    wait_for(md, load_sem.at[2])
-    wait_for(ed, load_sem.at[3])
+    send_vec = to_peer(vec, got_vec, small_sem.at[4], more_sem.at[2])
+
+    wait_for(other_d, load_sem.at[1])
     acc_d[...] = jnp.zeros_like(acc_d)
+    acc_o[...] = jnp.zeros_like(acc_o)
 
     def eighths(x):
         return jnp.sum(x.reshape(step_d // 8, 8, cols), axis=0)
@@ -279,49 +302,63 @@
         acc_d[...] += eighths(x * x)
 
     slot_d = me * n + here
-    stat_d[pl.ds(slot_d, 1), 0:1, :] = jnp.sum(acc_d[...], axis=0).reshape(1, 1, cols)
+    stat_d[pl.ds(slot_d, 1), :, :] = jnp.broadcast_to(jnp.sum(acc_d[...], axis=0).reshape(1, 1, cols), (1, 4, cols))
     acc_d[...] = jnp.zeros_like(acc_d)
-    wait_for(eu, load_sem.at[5])
+    wait_for(other_d, load_sem.at[2])
 
     @blocks(rows - first, step_u)
     def _(at):
         span = pl.ds(pl.multiple_of(first + at, step_u), step_u)
         base_u[pl.ds(at, step_u), :] = mu[span, :] - (learn_rate * hold_rate) * eu[span, :]
 
-    wait_for(own_d, load_sem.at[4])
-    to_peer(own_u.at[rest, :], other_u.at[0], 3, more_sem.at[0])
-    to_peer(base_u, other_u.at[1], 3, more_sem.at[0])
-    to_peer(own_d, other_d.at[0], 4, more_sem.at[1])
-    to_peer(base_d, other_d.at[1], 4, more_sem.at[1])
-
-    for group in range(1, groups - 1):
-        sum_rows(group)
+    to_peer(own_u.at[rest, :], other_u.at[0], send_sem.at[0], more_sem.at[0])
+    to_peer(base_u, other_u.at[1], send_sem.at[0], more_sem.at[0])
+
+    @pl.when(me == 0)
+    def _():
+        to_peer(own_d.at[head, :], other_d.at[0, head, :], send_sem.at[0], more_sem.at[1])
+
     @pl.when(me == 1)
     def _():
-        pl.semaphore_wait(barrier, n - 1)
-        pl.semaphore_signal(ready, inc=1, device_id={"dp": peer})
-
-    @pl.when(me == 0)
-    def _():
-        pl.semaphore_wait(ready, 1)
-
-    for group in range(groups - 1):
-        send_sizes(group)
+        to_peer(own_d, other_d.at[0], send_sem.at[0], more_sem.at[1])
+        to_peer(pd.at[last, columns(peer)], sum_d.at[last, :], send_sem.at[0], part_sem.at[groups + 2])
+
+    to_peer(base_d, other_d.at[1], send_sem.at[0], more_sem.at[4])
+
+    @pl.when(2 * here < n)
+    def _():
+        meet()
+        for group in range(groups - 1):
+            send_sizes(group)
+
     sum_rows(groups - 1)
     send_sizes(groups - 1)
 
-    for chunk, part in enumerate(spans_d):
-        sent[groups + chunk].wait_recv()
-
+    def sum_columns(part, acc, one, two, total=None):
         @blocks(part.size, step_d)
         def _(at):
             span = pl.ds(pl.multiple_of(part.start + at, step_d), step_d)
-            x = own_d[span, :] + sum_d[span, :]
-            sum_d[span, :] = x
-            acc_d[...] += eighths(x * x)
+            x = one[span, :] + two[span, :]
+            if total is not None:
+                total[span, :] = x
+            if acc is not None:
+                acc[...] += eighths(x * x)
+
+    wait_for(give_d, load_sem.at[0])
+    for at, span in enumerate(heads):
+        sent[groups + at].wait_recv()
+        sum_columns(span, acc_d, own_d, sum_d, sum_d)
+
+    @pl.when(me == 1)
+    def _():
+        wait_for(sum_d.at[last, :], part_sem.at[groups + 2])
+        sum_columns(last, acc_d, own_d, sum_d, sum_d)
+        wait_for(sum_d.at[last, :], part_sem.at[groups + 3])
+        sum_columns(last, acc_o, give_d, other_d.at[0])
 
     stat_d[pl.ds(slot_d, 1), 1:2, :] = jnp.sum(acc_d[...], axis=0).reshape(1, 1, cols)
-    sizes(stat_d, slot_d, 5, stat_sem.at[groups], 2)
+    stat_d[pl.ds(slot_d, 1), 2:3, :] = jnp.sum(acc_o[...], axis=0).reshape(1, 1, cols)
+    sizes(stat_d, slot_d, 3, stat_sem.at[groups], 2)
 
     for group in range(groups):
         span = spans_u[group]
@@ -349,11 +386,11 @@
                 cu[pl.ds(pl.multiple_of(me * rows + start, step_u), step_u), :] = stepped.astype(cu.dtype)
 
             part = cu.at[at_core(me, rows, group * lanes, lanes), :]
-            to_peer(part, part, 7, more_sem.at[3])
+            to_peer(part, part, send_sem.at[0], more_sem.at[3])
         else:
             if group == gathered:
                 wait_for(other_u, more_sem.at[0])
-                wait_for(give_u, load_sem.at[6])
+                wait_for(give_u, small_sem.at[0])
 
             @blocks(lanes, step_u // 2)
             def _(at):
@@ -389,23 +426,30 @@
         )
         rounded[...] = whole.reshape(rounded.shape).astype(rounded.dtype)
 
-    wait_for(give_d, load_sem.at[7])
-    wait_for(other_d, more_sem.at[1])
-    wait_for(other_d, send_sem.at[0])
-    wait_for(other_u, send_sem.at[3])
-    wait_for(other_d, send_sem.at[4])
+    @pl.when(me == 0)
+    def _():
+        wait_for(sum_d.at[last, :], part_sem.at[groups + 2])
+        sum_columns(last, None, own_d, sum_d, sum_d)
+        wait_for(pack.at[0], more_sem.at[1])
+
+    @pl.when(me == 1)
+    def _():
+        wait_for(pack.at[0, head, :], more_sem.at[1])
+
+    wait_for(base_d, more_sem.at[4])
+
     send_vec.wait_send()
-    wait_for(stat_u.at[pl.ds(0, gathered * (n - 1))], send_sem.at[1])
-    wait_for(stat_w.at[pl.ds(0, (groups - gathered) * (2 * n - 1))], send_sem.at[2])
+    wait_for(stat_u.at[pl.ds(0, gathered * (n - 1))], small_sem.at[1])
+    wait_for(stat_w.at[pl.ds(0, (groups - gathered) * (2 * n - 1))], small_sem.at[2])
     wait_for(stat_d.at[pl.ds(0, 2 * n - 1)], stat_sem.at[groups])
-    wait_for(stat_d.at[pl.ds(0, 2 * n - 1)], send_sem.at[5])
+    wait_for(stat_d.at[pl.ds(0, 2 * n - 1)], small_sem.at[3])
     wait_for(cu.at[at_core(peer, rows, 0, first), :], more_sem.at[3])
-    wait_for(cu.at[at_core(me, rows, 0, first), :], send_sem.at[7])
+    wait_for(pack, send_sem.at[0])
 
 
 def finish(
     cu_v, cn_v, cb_v, su_v, sn_v, sb_v, tu_v, tn_v, tb_v,
-    sum_d, base_d, ed, give_d, other_d, stat_d,
+    pack, ed, stat_d,
     cu, cd, cn, cb, su, sd, sn, sb, tu, td, tn, tb,
     cd_v, sd_v, td_v, sem,
 ):
@@ -414,6 +458,7 @@
     n = lax.axis_size("tp")
     tall, cols = td_v.shape
     step = 32
+    mine_d, base_o, sum_d, base_d, give_d = (pack.at[at] for at in range(5))
 
     def out(source, target, at):
         copy = pltpu.make_async_copy(source, target, sem.at[at])
@@ -421,7 +466,7 @@
         return copy
 
     small = [
-        out(source, target, 4 + at)
+        out(source, target, 2 + at)
         for at, (source, target) in enumerate(
             ((cn_v, cn), (cb_v, cb), (sn_v, sn), (sb_v, sb), (tn_v, tn), (tb_v, tb))
         )
@@ -430,7 +475,15 @@
     out(tu_v, tu, 0)
     out(cu_v, cu, 1)
 
-    own, other = (scale_at(stat_d, core * n, n, rate) for core in (me, 1 - me))
+    scales = []
+    for core in (me, 1 - me):
+        weights = sizes = 0.0
+        for at in range(n):
+            near, far = stat_d[core * n + at], stat_d[(1 - core) * n + at]
+            weights = weights + near[0:1, :]
+            sizes = sizes + near[1:2, :] + far[2:3, :]
+        scales.append(scale_of(weights, sizes, rate))
+    own, other = scales
     for piece in range(pieces):
         size = tall // pieces
 
@@ -442,20 +495,18 @@
             stepped = base_d[span, :] - learn_rate * x
             sd_v[span, :] = stepped
             cd_v[span, pl.ds(pl.multiple_of(me * cols, cols), cols)] = stepped.astype(cd_v.dtype)
-            x = (give_d[span, :] + other_d[0, span, :]) * other
-            stepped = other_d[1, span, :] - learn_rate * x
+            x = (give_d[span, :] + mine_d[span, :]) * other
+            stepped = base_o[span, :] - learn_rate * x
             cd_v[span, pl.ds(pl.multiple_of((1 - me) * cols, cols), cols)] = stepped.astype(cd_v.dtype)
 
         span = pl.ds(piece * size, size)
-        out(td_v.at[span, :], td.at[span, :], 2)
-        out(sd_v.at[span, :], sd.at[span, :], 2)
-        out(cd_v.at[span, :], cd.at[span, :], 3)
+        out(td_v.at[span, :], td.at[span, :], 0)
+        out(sd_v.at[span, :], sd.at[span, :], 0)
+        out(cd_v.at[span, :], cd.at[span, :], 0)
     for copy in small:
         copy.wait()
-    wait_for(other_d, sem.at[0])
     wait_for(cu_v, sem.at[1])
-    wait_for(other_d, sem.at[2])
-    wait_for(cd_v, sem.at[3])
+    wait_for(pack, sem.at[0])
 
 
 def held(arrays):
@@ -481,9 +532,9 @@
         shaped((pu.shape[1], wide), bf16), shaped((pn.shape[1],), bf16), shaped((pb.shape[1],), bf16),
         *(shaped(x.shape) for x in (mu, mn, mb)),
         *(shaped(x.shape) for x in (mu, mn, mb)),
-        *(shaped(md.shape) for _ in range(4)),
-        shaped((2, *md.shape)),
-        shaped((2 * n, 2, cols)),
+        shaped((5, *md.shape)),
+        shaped(md.shape),
+        shaped((2 * n, 4, cols)),
     ]
     results = pl.pallas_call(
         exchange,
@@ -504,14 +555,15 @@
             pltpu.VMEM((rows, lanes), f32),
             pltpu.VMEM((rest, lanes), f32),
             pltpu.VMEM((8, cols), f32),
+            pltpu.VMEM((8, cols), f32),
             pltpu.VMEM((gathered * n, 2, lanes), f32),
             pltpu.VMEM(((groups - gathered) * 2 * n, 2, lanes), f32),
-            dma((8,)),
+            dma((3,)),
             dma((6,)),
-            dma((groups + 2,)),
-            dma((8,)),
+            dma((groups + 4,)),
+            dma((1,)),
             dma((groups + 1,)),
-            dma((4,)),
+            dma((5,)),
             pltpu.SemaphoreType.REGULAR,
             pltpu.SemaphoreType.REGULAR,
         ],
@@ -537,7 +589,7 @@
             pltpu.VMEM((tall, pd.shape[2]), bf16),
             pltpu.VMEM(md.shape, f32),
             pltpu.VMEM(md.shape, f32),
-            dma((10,)),
+            dma((8,)),
         ],
         compiler_params=pltpu.CompilerParams(vmem_limit_bytes=8 * 2**20),
         name="finish",

time: 15.7 us -> 15.4 us (0.981)
  Pallas kernels: 14.9 us -> 14.6 us
    pallas_call x1, Pallas kernels: 11.9 us -> 11.6 us  [on_pair(): pl.pallas_call(exchange, out_shape=between, in_specs=[hbm] * len(args), o...]
where the time goes in v2:
time: 15.4 us; the launch traced here: 15.2 us
  Pallas kernels  14.6 us (95%)
  between operations  0.66 us (4%)
    pallas_call x1, Pallas kernels, on_pair(): pl.pallas_call(exchange, out_shape=between, in_specs=[hbm] * len(args), o...  11.6 us
    pallas_call x1, Pallas kernels, on_pair(): pl.pallas_call(finish, out_shape=[shaped(shape, dtype) for shape, dtype i...  2.98 us

profile of v2, /device:TPU:0, one launch (start us, length us, event | category | flops | bytes accessed | tf_op | source)
XLA Modules:
  0.0 15.2 jit_solution(271526602355289653)
XLA Ops:
  0.6 11.6 %exchange.1 = (bf16[768,768]{1,0:T(8,128)(2,1)S(1)}, bf16[768]{0:T(1024)(128)(2,1)S(1)}, bf16[768]{0:T(1024)(128)(2,1)S(1)}, f32[384,768]{1,0:T(8,128)S(1)}, f32...) custom-call(f32[768,768]{1,0:T(8,128)} %bitcast.2, ...), custom_call_target="tpu_custom_call" | custom-call | tf_op jit(solution)/shard_map/exchange/pallas_call | solution.py:539
  12.2 3.0 %finish.1 = (bf16[768,768]{1,0:T(8,128)(2,1)}, bf16[768,768]{1,0:T(8,128)(2,1)}, bf16[768]{0:T(1024)(128)(2,1)}, bf16[768]{0:T(1024)(128)(2,1)}, f32[384,768]{1,...) custom-call(bf16[768,768]{1,0:T(8,128)(2,1)S(1)} %get-tuple-element., ...), custom_call_target="tpu_custom_call" | custom-call | tf_op jit(solution)/shard_map/finish/pallas_call | solution.py:583

commit v3 on v2

--- a/solution.py
+++ b/solution.py
@@ -119,14 +119,26 @@
     return scale_of(total[0:1, :], total[1:2, :], rate)
 
 
-def exchange(
+def exchange(*refs):
+    (*refs, last_sem), stat_d = refs, refs[23]
+    n = stat_d.shape[0] // 2
+    groups = refs[4].shape[0] // lanes
+    dma, regular = pltpu.SemaphoreType.DMA, pltpu.SemaphoreType.REGULAR
+    pl.run_scoped(
+        functools.partial(exchange_all_but_last, *refs, last_sem),
+        dma((2,)), dma((6,)), dma((groups + 4,)), dma((1,)), dma((groups,)), dma((5,)), regular, regular,
+    )
+    wait_for(stat_d.at[pl.ds(0, 2 * n - 1)], last_sem.at[0])
+
+
+def exchange_all_but_last(
     pu, pd, pn, pb, mu_h, md_h, mn, mb, eu_h, ed_h, en, eb,
     cu, cn, cb, su, sn, sb, tu, tn, tb,
     pack, ed, stat_d,
     own_u, own_d, give_u, sum_u, base_u, other_u, mu, md, eu,
     pn_v, pb_v, mn_v, mb_v, en_v, eb_v, vec, got_vec,
     sq_u, sq_o, acc_d, acc_o, stat_u, stat_w,
-    load_sem, small_sem, part_sem, send_sem, stat_sem, more_sem, hello, ready,
+    last_sem, load_sem, small_sem, part_sem, send_sem, stat_sem, more_sem, hello, ready,
 ):
     me = lax.axis_index("dp")
     peer = 1 - me
@@ -203,8 +215,8 @@
 
     load(md_h, md, load_sem.at[1])
     load(ed_h, ed, load_sem.at[1])
-    load(eu_h, eu, load_sem.at[2])
-    load(pd.at[:, columns(me)], own_d, load_sem.at[2])
+    load(eu_h, eu, load_sem.at[1])
+    load(pd.at[:, columns(me)], own_d, load_sem.at[1])
 
     wait_for(other_d, load_sem.at[0])
     load(pd.at[:, columns(peer)], give_d, load_sem.at[0])
@@ -230,15 +242,16 @@
         store_size(group, 0)
 
     def sizes(ref, at, send, recv, cores):
-        for step in range(n):
+        for step in (*range(1, n), 0):
             for core in range(cores):
                 if step + core > 0:
+                    target = me if cores == 1 else core if step else peer
                     pltpu.make_async_remote_copy(
                         src_ref=ref.at[at],
                         dst_ref=ref.at[at],
                         send_sem=small_sem.at[send],
                         recv_sem=recv,
-                        device_id={"dp": peer if core else me, "tp": lax.rem(here + step, n)},
+                        device_id={"dp": target, "tp": lax.rem(here + step, n)},
                     ).start()
 
     def sum_rows(group):
@@ -287,7 +300,7 @@
     vec[3:4, half:] = eb_v[...].reshape(1, half)
     send_vec = to_peer(vec, got_vec, small_sem.at[4], more_sem.at[2])
 
-    wait_for(other_d, load_sem.at[1])
+    wait_for(pack.at[pl.ds(0, 4)], load_sem.at[1])
     acc_d[...] = jnp.zeros_like(acc_d)
     acc_o[...] = jnp.zeros_like(acc_o)
 
@@ -304,7 +317,6 @@
     slot_d = me * n + here
     stat_d[pl.ds(slot_d, 1), :, :] = jnp.broadcast_to(jnp.sum(acc_d[...], axis=0).reshape(1, 1, cols), (1, 4, cols))
     acc_d[...] = jnp.zeros_like(acc_d)
-    wait_for(other_d, load_sem.at[2])
 
     @blocks(rows - first, step_u)
     def _(at):
@@ -358,7 +370,7 @@
 
     stat_d[pl.ds(slot_d, 1), 1:2, :] = jnp.sum(acc_d[...], axis=0).reshape(1, 1, cols)
     stat_d[pl.ds(slot_d, 1), 2:3, :] = jnp.sum(acc_o[...], axis=0).reshape(1, 1, cols)
-    sizes(stat_d, slot_d, 3, stat_sem.at[groups], 2)
+    sizes(stat_d, slot_d, 3, last_sem.at[0], 2)
 
     for group in range(groups):
         span = spans_u[group]
@@ -441,7 +453,6 @@
     send_vec.wait_send()
     wait_for(stat_u.at[pl.ds(0, gathered * (n - 1))], small_sem.at[1])
     wait_for(stat_w.at[pl.ds(0, (groups - gathered) * (2 * n - 1))], small_sem.at[2])
-    wait_for(stat_d.at[pl.ds(0, 2 * n - 1)], stat_sem.at[groups])
     wait_for(stat_d.at[pl.ds(0, 2 * n - 1)], small_sem.at[3])
     wait_for(cu.at[at_core(peer, rows, 0, first), :], more_sem.at[3])
     wait_for(pack, send_sem.at[0])
@@ -465,46 +476,54 @@
         copy.start()
         return copy
 
-    small = [
-        out(source, target, 2 + at)
-        for at, (source, target) in enumerate(
-            ((cn_v, cn), (cb_v, cb), (sn_v, sn), (sb_v, sb), (tn_v, tn), (tb_v, tb))
-        )
-    ]
-    out(su_v, su, 0)
-    out(tu_v, tu, 0)
-    out(cu_v, cu, 1)
-
-    scales = []
-    for core in (me, 1 - me):
-        weights = sizes = 0.0
-        for at in range(n):
-            near, far = stat_d[core * n + at], stat_d[(1 - core) * n + at]
-            weights = weights + near[0:1, :]
-            sizes = sizes + near[1:2, :] + far[2:3, :]
-        scales.append(scale_of(weights, sizes, rate))
-    own, other = scales
-    for piece in range(pieces):
-        size = tall // pieces
-
-        @blocks(size, step)
-        def _(at):
-            span = pl.ds(pl.multiple_of(piece * size + at, step), step)
-            x = sum_d[span, :] * own
-            td_v[span, :] = hold_rate * ed[span, :] + x
-            stepped = base_d[span, :] - learn_rate * x
-            sd_v[span, :] = stepped
-            cd_v[span, pl.ds(pl.multiple_of(me * cols, cols), cols)] = stepped.astype(cd_v.dtype)
-            x = (give_d[span, :] + mine_d[span, :]) * other
-            stepped = base_o[span, :] - learn_rate * x
-            cd_v[span, pl.ds(pl.multiple_of((1 - me) * cols, cols), cols)] = stepped.astype(cd_v.dtype)
-
-        span = pl.ds(piece * size, size)
-        out(td_v.at[span, :], td.at[span, :], 0)
-        out(sd_v.at[span, :], sd.at[span, :], 0)
-        out(cd_v.at[span, :], cd.at[span, :], 0)
-    for copy in small:
-        copy.wait()
+    def vectors(small_sem):
+        small = [
+            pltpu.make_async_copy(source, target, small_sem.at[at])
+            for at, (source, target) in enumerate(
+                ((cn_v, cn), (cb_v, cb), (sn_v, sn), (sb_v, sb), (tn_v, tn), (tb_v, tb))
+            )
+        ]
+        for copy in small:
+            copy.start()
+        matrices()
+        for copy in small:
+            copy.wait()
+
+    def matrices():
+        out(su_v, su, 0)
+        out(tu_v, tu, 0)
+        out(cu_v, cu, 1)
+
+        scales = []
+        for core in (me, 1 - me):
+            weights = sizes = 0.0
+            for at in range(n):
+                near, far = stat_d[core * n + at], stat_d[(1 - core) * n + at]
+                weights = weights + near[0:1, :]
+                sizes = sizes + near[1:2, :] + far[2:3, :]
+            scales.append(scale_of(weights, sizes, rate))
+        own, other = scales
+        for piece in range(pieces):
+            size = tall // pieces
+
+            @blocks(size, step)
+            def _(at):
+                span = pl.ds(pl.multiple_of(piece * size + at, step), step)
+                x = sum_d[span, :] * own
+                td_v[span, :] = hold_rate * ed[span, :] + x
+                stepped = base_d[span, :] - learn_rate * x
+                sd_v[span, :] = stepped
+                cd_v[span, pl.ds(pl.multiple_of(me * cols, cols), cols)] = stepped.astype(cd_v.dtype)
+                x = (give_d[span, :] + mine_d[span, :]) * other
+                stepped = base_o[span, :] - learn_rate * x
+                cd_v[span, pl.ds(pl.multiple_of((1 - me) * cols, cols), cols)] = stepped.astype(cd_v.dtype)
+
+            span = pl.ds(piece * size, size)
+            out(td_v.at[span, :], td.at[span, :], 0)
+            out(sd_v.at[span, :], sd.at[span, :], 0)
+            out(cd_v.at[span, :], cd.at[span, :], 0)
+
+    pl.run_scoped(vectors, pltpu.SemaphoreType.DMA((6,)))
     wait_for(cu_v, sem.at[1])
     wait_for(pack, sem.at[0])
 
@@ -558,14 +577,7 @@
             pltpu.VMEM((8, cols), f32),
             pltpu.VMEM((gathered * n, 2, lanes), f32),
             pltpu.VMEM(((groups - gathered) * 2 * n, 2, lanes), f32),
-            dma((3,)),
-            dma((6,)),
-            dma((groups + 4,)),
             dma((1,)),
-            dma((groups + 1,)),
-            dma((5,)),
-            pltpu.SemaphoreType.REGULAR,
-            pltpu.SemaphoreType.REGULAR,
         ],
         compiler_params=pltpu.CompilerParams(
             collective_id=0, has_side_effects=True, vmem_limit_bytes=40 * 2**20
@@ -589,7 +601,7 @@
             pltpu.VMEM((tall, pd.shape[2]), bf16),
             pltpu.VMEM(md.shape, f32),
             pltpu.VMEM(md.shape, f32),
-            dma((8,)),
+            dma((2,)),
         ],
         compiler_params=pltpu.CompilerParams(vmem_limit_bytes=8 * 2**20),
         name="finish",

time: 15.4 us -> 15.1 us (0.981)
  Pallas kernels: 14.6 us -> 14.3 us
    pallas_call x1, Pallas kernels: 11.6 us -> 11.3 us  [on_pair(): pl.pallas_call(exchange, out_shape=between, in_specs=[hbm] * len(args), o...]
where the time goes in v3:
time: 15.1 us; the launch traced here: 14.9 us
  Pallas kernels  14.3 us (95%)
  between operations  0.66 us (4%)
    pallas_call x1, Pallas kernels, on_pair(): pl.pallas_call(exchange, out_shape=between, in_specs=[hbm] * len(args), o...  11.3 us
    pallas_call x1, Pallas kernels, on_pair(): pl.pallas_call(finish, out_shape=[shaped(shape, dtype) for shape, dtype i...  2.94 us

profile of v3, /device:TPU:0, one launch (start us, length us, event | category | flops | bytes accessed | tf_op | source)
XLA Modules:
  0.0 14.9 jit_solution(4550216931695073672)
XLA Ops:
  0.6 11.3 %exchange.1 = (bf16[768,768]{1,0:T(8,128)(2,1)S(1)}, bf16[768]{0:T(1024)(128)(2,1)S(1)}, bf16[768]{0:T(1024)(128)(2,1)S(1)}, f32[384,768]{1,0:T(8,128)S(1)}, f32...) custom-call(f32[768,768]{1,0:T(8,128)} %bitcast.2, ...), custom_call_target="tpu_custom_call" | custom-call | tf_op jit(solution)/shard_map/exchange/pallas_call | solution.py:558
  12.0 2.9 %finish.1 = (bf16[768,768]{1,0:T(8,128)(2,1)}, bf16[768,768]{1,0:T(8,128)(2,1)}, bf16[768]{0:T(1024)(128)(2,1)}, bf16[768]{0:T(1024)(128)(2,1)}, f32[384,768]{1,...) custom-call(bf16[768,768]{1,0:T(8,128)(2,1)S(1)} %get-tuple-element., ...), custom_call_target="tpu_custom_call" | custom-call | tf_op jit(solution)/shard_map/finish/pallas_call | solution.py:595

commit v4 on v3

--- a/solution.py
+++ b/solution.py
@@ -120,25 +120,22 @@
 
 
 def exchange(*refs):
-    (*refs, last_sem), stat_d = refs, refs[23]
-    n = stat_d.shape[0] // 2
     groups = refs[4].shape[0] // lanes
     dma, regular = pltpu.SemaphoreType.DMA, pltpu.SemaphoreType.REGULAR
     pl.run_scoped(
-        functools.partial(exchange_all_but_last, *refs, last_sem),
-        dma((2,)), dma((6,)), dma((groups + 4,)), dma((1,)), dma((groups,)), dma((5,)), regular, regular,
-    )
-    wait_for(stat_d.at[pl.ds(0, 2 * n - 1)], last_sem.at[0])
-
-
-def exchange_all_but_last(
+        functools.partial(exchange_in_scope, *refs),
+        dma((2,)), dma((6,)), dma((groups + 7,)), dma((1,)), dma((groups + 1,)), dma((5,)), regular, regular,
+    )
+
+
+def exchange_in_scope(
     pu, pd, pn, pb, mu_h, md_h, mn, mb, eu_h, ed_h, en, eb,
     cu, cn, cb, su, sn, sb, tu, tn, tb,
     pack, ed, stat_d,
     own_u, own_d, give_u, sum_u, base_u, other_u, mu, md, eu,
     pn_v, pb_v, mn_v, mb_v, en_v, eb_v, vec, got_vec,
     sq_u, sq_o, acc_d, acc_o, stat_u, stat_w,
-    last_sem, load_sem, small_sem, part_sem, send_sem, stat_sem, more_sem, hello, ready,
+    load_sem, small_sem, part_sem, send_sem, stat_sem, more_sem, hello, ready,
 ):
     me = lax.axis_index("dp")
     peer = 1 - me
@@ -149,7 +146,7 @@
     tall, cols = md.shape
     groups = rows // lanes
     step_u, step_d = 32, 64
-    shared = tall // 6 // step_d * step_d
+    shared = 5 * tall // 24 // 32 * 32
     other_d, (sum_d, base_d, give_d) = pack.at[pl.ds(0, 2)], (pack.at[at] for at in range(2, 5))
     first = gathered * lanes
     rest = pl.ds(first, rows - first)
@@ -198,9 +195,13 @@
         copy.start()
         return copy
 
+    def ending(start, size):
+        return [pl.ds(start, size - step_u), pl.ds(start + size - step_u, step_u)]
+
     spans_u = [pl.ds(at * lanes, lanes) for at in range(groups)]
     head, last = pl.ds(0, tall - shared), pl.ds(tall - shared, shared)
-    heads = pl.ds(0, tall - 2 * shared), pl.ds(tall - 2 * shared, shared)
+    heads = [pl.ds(0, tall - 2 * shared), *ending(tall - 2 * shared, shared)]
+    lasts = ending(tall - shared, shared)
     sent = [
         to_peer(pu.at[at_core(peer, rows, at * lanes, lanes), :], sum_u.at[span, :], send_sem.at[0], part_sem.at[at])
         for at, span in enumerate(spans_u)
@@ -210,8 +211,10 @@
 
     @pl.when(me == 0)
     def _():
-        to_peer(pd.at[last, columns(peer)], sum_d.at[last, :], send_sem.at[0], part_sem.at[groups + 2])
-        to_peer(pd.at[last, columns(me)], other_d.at[0, last, :], send_sem.at[0], part_sem.at[groups + 3])
+        for at, span in enumerate(lasts):
+            to_peer(pd.at[span, columns(peer)], sum_d.at[span, :], send_sem.at[0], part_sem.at[groups + 3 + at])
+        for at, span in enumerate(lasts):
+            to_peer(pd.at[span, columns(me)], other_d.at[0, span, :], send_sem.at[0], part_sem.at[groups + 5 + at])
 
     load(md_h, md, load_sem.at[1])
     load(ed_h, ed, load_sem.at[1])
@@ -305,7 +308,7 @@
     acc_o[...] = jnp.zeros_like(acc_o)
 
     def eighths(x):
-        return jnp.sum(x.reshape(step_d // 8, 8, cols), axis=0)
+        return jnp.sum(x.reshape(x.shape[0] // 8, 8, cols), axis=0)
 
     @blocks(tall, step_d)
     def _(at):
@@ -333,7 +336,7 @@
     @pl.when(me == 1)
     def _():
         to_peer(own_d, other_d.at[0], send_sem.at[0], more_sem.at[1])
-        to_peer(pd.at[last, columns(peer)], sum_d.at[last, :], send_sem.at[0], part_sem.at[groups + 2])
+        to_peer(pd.at[last, columns(peer)], sum_d.at[last, :], send_sem.at[0], part_sem.at[groups + 3])
 
     to_peer(base_d, other_d.at[1], send_sem.at[0], more_sem.at[4])
 
@@ -347,9 +350,11 @@
     send_sizes(groups - 1)
 
     def sum_columns(part, acc, one, two, total=None):
-        @blocks(part.size, step_d)
+        step = step_d if part.size % step_d == 0 else 32
+
+        @blocks(part.size, step)
         def _(at):
-            span = pl.ds(pl.multiple_of(part.start + at, step_d), step_d)
+            span = pl.ds(pl.multiple_of(part.start + at, 32), step)
             x = one[span, :] + two[span, :]
             if total is not None:
                 total[span, :] = x
@@ -363,14 +368,16 @@
 
     @pl.when(me == 1)
     def _():
-        wait_for(sum_d.at[last, :], part_sem.at[groups + 2])
-        sum_columns(last, acc_d, own_d, sum_d, sum_d)
-        wait_for(sum_d.at[last, :], part_sem.at[groups + 3])
-        sum_columns(last, acc_o, give_d, other_d.at[0])
+        for at, span in enumerate(lasts):
+            wait_for(sum_d.at[span, :], part_sem.at[groups + 3 + at])
+            sum_columns(span, acc_d, own_d, sum_d, sum_d)
+        for at, span in enumerate(lasts):
+            wait_for(sum_d.at[span, :], part_sem.at[groups + 5 + at])
+            sum_columns(span, acc_o, give_d, other_d.at[0])
 
     stat_d[pl.ds(slot_d, 1), 1:2, :] = jnp.sum(acc_d[...], axis=0).reshape(1, 1, cols)
     stat_d[pl.ds(slot_d, 1), 2:3, :] = jnp.sum(acc_o[...], axis=0).reshape(1, 1, cols)
-    sizes(stat_d, slot_d, 3, last_sem.at[0], 2)
+    sizes(stat_d, slot_d, 3, stat_sem.at[groups], 2)
 
     for group in range(groups):
         span = spans_u[group]
@@ -440,7 +447,7 @@
 
     @pl.when(me == 0)
     def _():
-        wait_for(sum_d.at[last, :], part_sem.at[groups + 2])
+        wait_for(sum_d.at[last, :], part_sem.at[groups + 3])
         sum_columns(last, None, own_d, sum_d, sum_d)
         wait_for(pack.at[0], more_sem.at[1])
 
@@ -454,6 +461,7 @@
     wait_for(stat_u.at[pl.ds(0, gathered * (n - 1))], small_sem.at[1])
     wait_for(stat_w.at[pl.ds(0, (groups - gathered) * (2 * n - 1))], small_sem.at[2])
     wait_for(stat_d.at[pl.ds(0, 2 * n - 1)], small_sem.at[3])
+    wait_for(stat_d.at[pl.ds(0, 2 * n - 1)], stat_sem.at[groups])
     wait_for(cu.at[at_core(peer, rows, 0, first), :], more_sem.at[3])
     wait_for(pack, send_sem.at[0])
 
@@ -462,7 +470,7 @@
     cu_v, cn_v, cb_v, su_v, sn_v, sb_v, tu_v, tn_v, tb_v,
     pack, ed, stat_d,
     cu, cd, cn, cb, su, sd, sn, sb, tu, td, tn, tb,
-    cd_v, sd_v, td_v, sem,
+    cd_v, sd_v, td_v,
 ):
     me = lax.axis_index("dp")
     rate = lax.axis_size("dp") ** (-0.5)
@@ -471,28 +479,30 @@
     step = 32
     mine_d, base_o, sum_d, base_d, give_d = (pack.at[at] for at in range(5))
 
-    def out(source, target, at):
-        copy = pltpu.make_async_copy(source, target, sem.at[at])
+    def out(source, target, sem):
+        copy = pltpu.make_async_copy(source, target, sem)
         copy.start()
         return copy
 
-    def vectors(small_sem):
+    def write(sem):
         small = [
-            pltpu.make_async_copy(source, target, small_sem.at[at])
+            pltpu.make_async_copy(source, target, sem.at[2 + at])
             for at, (source, target) in enumerate(
                 ((cn_v, cn), (cb_v, cb), (sn_v, sn), (sb_v, sb), (tn_v, tn), (tb_v, tb))
             )
         ]
         for copy in small:
             copy.start()
-        matrices()
+        matrices(sem)
         for copy in small:
             copy.wait()
-
-    def matrices():
-        out(su_v, su, 0)
-        out(tu_v, tu, 0)
-        out(cu_v, cu, 1)
+        wait_for(cu_v, sem.at[1])
+        wait_for(pack, sem.at[0])
+
+    def matrices(sem):
+        out(su_v, su, sem.at[0])
+        out(tu_v, tu, sem.at[0])
+        out(cu_v, cu, sem.at[1])
 
         scales = []
         for core in (me, 1 - me):
@@ -519,13 +529,11 @@
                 cd_v[span, pl.ds(pl.multiple_of((1 - me) * cols, cols), cols)] = stepped.astype(cd_v.dtype)
 
             span = pl.ds(piece * size, size)
-            out(td_v.at[span, :], td.at[span, :], 0)
-            out(sd_v.at[span, :], sd.at[span, :], 0)
-            out(cd_v.at[span, :], cd.at[span, :], 0)
-
-    pl.run_scoped(vectors, pltpu.SemaphoreType.DMA((6,)))
-    wait_for(cu_v, sem.at[1])
-    wait_for(pack, sem.at[0])
+            out(td_v.at[span, :], td.at[span, :], sem.at[0])
+            out(sd_v.at[span, :], sd.at[span, :], sem.at[0])
+            out(cd_v.at[span, :], cd.at[span, :], sem.at[0])
+
+    pl.run_scoped(write, pltpu.SemaphoreType.DMA((8,)))
 
 
 def held(arrays):
@@ -542,7 +550,6 @@
     rows, cols = mu.shape[0], md.shape[1]
     groups = rows // lanes
     rest = rows - gathered * lanes
-    dma = pltpu.SemaphoreType.DMA
 
     def shaped(shape, dtype=f32):
         return jax.ShapeDtypeStruct(shape, dtype)
@@ -577,7 +584,6 @@
             pltpu.VMEM((8, cols), f32),
             pltpu.VMEM((gathered * n, 2, lanes), f32),
             pltpu.VMEM(((groups - gathered) * 2 * n, 2, lanes), f32),
-            dma((1,)),
         ],
         compiler_params=pltpu.CompilerParams(
             collective_id=0, has_side_effects=True, vmem_limit_bytes=40 * 2**20
@@ -601,7 +607,6 @@
             pltpu.VMEM((tall, pd.shape[2]), bf16),
             pltpu.VMEM(md.shape, f32),
             pltpu.VMEM(md.shape, f32),
-            dma((2,)),
         ],
         compiler_params=pltpu.CompilerParams(vmem_limit_bytes=8 * 2**20),
         name="finish",

time: 15.1 us -> 15 us (level)
  no operation moved by 1% of the time
where the time goes in v4:
time: 15 us; the launch traced here: 14.8 us
  Pallas kernels  14.2 us (95%)
  between operations  0.65 us (4%)
    pallas_call x1, Pallas kernels, on_pair(): pl.pallas_call(exchange, out_shape=between, in_specs=[hbm] * len(args), o...  11.3 us
    pallas_call x1, Pallas kernels, on_pair(): pl.pallas_call(finish, out_shape=[shaped(shape, dtype) for shape, dtype i...  2.9 us

profile of v4, /device:TPU:0, one launch (start us, length us, event | category | flops | bytes accessed | tf_op | source)
XLA Modules:
  0.0 14.8 jit_solution(5827400849039099093)
XLA Ops:
  0.6 11.3 %exchange.1 = (bf16[768,768]{1,0:T(8,128)(2,1)S(1)}, bf16[768]{0:T(1024)(128)(2,1)S(1)}, bf16[768]{0:T(1024)(128)(2,1)S(1)}, f32[384,768]{1,0:T(8,128)S(1)}, f32...) custom-call(f32[768,768]{1,0:T(8,128)} %bitcast.2, ...), custom_call_target="tpu_custom_call" | custom-call | tf_op jit(solution)/shard_map/exchange/pallas_call | solution.py:565
  11.9 2.9 %finish.1 = (bf16[768,768]{1,0:T(8,128)(2,1)}, bf16[768,768]{1,0:T(8,128)(2,1)}, bf16[768]{0:T(1024)(128)(2,1)}, bf16[768]{0:T(1024)(128)(2,1)}, f32[384,768]{1,...) custom-call(bf16[768,768]{1,0:T(8,128)(2,1)S(1)} %get-tuple-element., ...), custom_call_target="tpu_custom_call" | custom-call | tf_op jit(solution)/shard_map/finish/pallas_call | solution.py:601

commit v5 on v4

--- a/solution.py
+++ b/solution.py
@@ -124,14 +124,14 @@
     dma, regular = pltpu.SemaphoreType.DMA, pltpu.SemaphoreType.REGULAR
     pl.run_scoped(
         functools.partial(exchange_in_scope, *refs),
-        dma((2,)), dma((6,)), dma((groups + 7,)), dma((1,)), dma((groups + 1,)), dma((5,)), regular, regular,
+        dma((2,)), dma((6,)), dma((groups + 7,)), dma((1,)), dma((groups + 2,)), dma((5,)), regular, regular,
     )
 
 
 def exchange_in_scope(
     pu, pd, pn, pb, mu_h, md_h, mn, mb, eu_h, ed_h, en, eb,
     cu, cn, cb, su, sn, sb, tu, tn, tb,
-    pack, ed, stat_d,
+    pack, ed, stat_d, stat_m,
     own_u, own_d, give_u, sum_u, base_u, other_u, mu, md, eu,
     pn_v, pb_v, mn_v, mb_v, en_v, eb_v, vec, got_vec,
     sq_u, sq_o, acc_d, acc_o, stat_u, stat_w,
@@ -162,6 +162,17 @@
         copy.start()
         return copy
 
+    barrier = pltpu.get_barrier_semaphore()
+
+    @pl.when(me == 1)
+    def _():
+        pl.semaphore_signal(barrier, inc=1, device_id={"dp": peer})
+
+    @pl.when(me == 0)
+    def _():
+        pl.semaphore_wait(barrier, 1)
+        pl.semaphore_signal(hello, inc=1, device_id={"dp": peer})
+
     small = [
         load(source, target, small_sem.at[at])
         for at, (source, target) in enumerate(
@@ -170,17 +181,6 @@
     ]
     load(pu.at[at_core(me, rows), :], own_u, load_sem.at[0])
     load(mu_h, mu, load_sem.at[0])
-
-    barrier = pltpu.get_barrier_semaphore()
-
-    @pl.when(me == 1)
-    def _():
-        pl.semaphore_signal(barrier, inc=1, device_id={"dp": peer})
-
-    @pl.when(me == 0)
-    def _():
-        pl.semaphore_wait(barrier, 1)
-        pl.semaphore_signal(hello, inc=1, device_id={"dp": peer})
 
     @pl.when(me == 1)
     def _():
@@ -306,6 +306,7 @@
     wait_for(pack.at[pl.ds(0, 4)], load_sem.at[1])
     acc_d[...] = jnp.zeros_like(acc_d)
     acc_o[...] = jnp.zeros_like(acc_o)
+    stat_d[pl.ds(me * n + here, 1), 1:2, :] = jnp.zeros((1, 1, cols), jnp.float32)
 
     def eighths(x):
         return jnp.sum(x.reshape(x.shape[0] // 8, 8, cols), axis=0)
@@ -318,7 +319,7 @@
         acc_d[...] += eighths(x * x)
 
     slot_d = me * n + here
-    stat_d[pl.ds(slot_d, 1), :, :] = jnp.broadcast_to(jnp.sum(acc_d[...], axis=0).reshape(1, 1, cols), (1, 4, cols))
+    stat_m[pl.ds(slot_d, 1), :, :] = jnp.sum(acc_d[...], axis=0).reshape(1, 1, cols)
     acc_d[...] = jnp.zeros_like(acc_d)
 
     @blocks(rows - first, step_u)
@@ -348,6 +349,7 @@
 
     sum_rows(groups - 1)
     send_sizes(groups - 1)
+    sizes(stat_m, slot_d, 5, stat_sem.at[groups + 1], 2)
 
     def sum_columns(part, acc, one, two, total=None):
         step = step_d if part.size % step_d == 0 else 32
@@ -366,17 +368,24 @@
         sent[groups + at].wait_recv()
         sum_columns(span, acc_d, own_d, sum_d, sum_d)
 
+    def store_total(acc, which):
+        stat_d[pl.ds(slot_d, 1), which : which + 1, :] = jnp.sum(acc[...], axis=0).reshape(1, 1, cols)
+
+    @pl.when(me == 0)
+    def _():
+        store_total(acc_d, 0)
+
     @pl.when(me == 1)
     def _():
         for at, span in enumerate(lasts):
             wait_for(sum_d.at[span, :], part_sem.at[groups + 3 + at])
             sum_columns(span, acc_d, own_d, sum_d, sum_d)
+        store_total(acc_d, 0)
         for at, span in enumerate(lasts):
             wait_for(sum_d.at[span, :], part_sem.at[groups + 5 + at])
             sum_columns(span, acc_o, give_d, other_d.at[0])
-
-    stat_d[pl.ds(slot_d, 1), 1:2, :] = jnp.sum(acc_d[...], axis=0).reshape(1, 1, cols)
-    stat_d[pl.ds(slot_d, 1), 2:3, :] = jnp.sum(acc_o[...], axis=0).reshape(1, 1, cols)
+        store_total(acc_o, 1)
+
     sizes(stat_d, slot_d, 3, stat_sem.at[groups], 2)
 
     for group in range(groups):
@@ -461,6 +470,8 @@
     wait_for(stat_u.at[pl.ds(0, gathered * (n - 1))], small_sem.at[1])
     wait_for(stat_w.at[pl.ds(0, (groups - gathered) * (2 * n - 1))], small_sem.at[2])
     wait_for(stat_d.at[pl.ds(0, 2 * n - 1)], small_sem.at[3])
+    wait_for(stat_m.at[pl.ds(0, 2 * n - 1)], small_sem.at[5])
+    wait_for(stat_m.at[pl.ds(0, 2 * n - 1)], stat_sem.at[groups + 1])
     wait_for(stat_d.at[pl.ds(0, 2 * n - 1)], stat_sem.at[groups])
     wait_for(cu.at[at_core(peer, rows, 0, first), :], more_sem.at[3])
     wait_for(pack, send_sem.at[0])
@@ -468,7 +479,7 @@
 
 def finish(
     cu_v, cn_v, cb_v, su_v, sn_v, sb_v, tu_v, tn_v, tb_v,
-    pack, ed, stat_d,
+    pack, ed, stat_d, stat_m,
     cu, cd, cn, cb, su, sd, sn, sb, tu, td, tn, tb,
     cd_v, sd_v, td_v,
 ):
@@ -509,8 +520,8 @@
             weights = sizes = 0.0
             for at in range(n):
                 near, far = stat_d[core * n + at], stat_d[(1 - core) * n + at]
-                weights = weights + near[0:1, :]
-                sizes = sizes + near[1:2, :] + far[2:3, :]
+                weights = weights + stat_m[core * n + at]
+                sizes = sizes + near[0:1, :] + far[1:2, :]
             scales.append(scale_of(weights, sizes, rate))
         own, other = scales
         for piece in range(pieces):
@@ -560,7 +571,8 @@
         *(shaped(x.shape) for x in (mu, mn, mb)),
         shaped((5, *md.shape)),
         shaped(md.shape),
-        shaped((2 * n, 4, cols)),
+        shaped((2 * n, 2, cols)),
+        shaped((2 * n, 1, cols)),
     ]
     results = pl.pallas_call(
         exchange,

time: 15 us -> 14.9 us (level)
  no operation moved by 1% of the time
where the time goes in v5:
time: 14.9 us; the launch traced here: 14.7 us
  Pallas kernels  14.1 us (95%)
  between operations  0.65 us (4%)
    pallas_call x1, Pallas kernels, on_pair(): pl.pallas_call(exchange, out_shape=between, in_specs=[hbm] * len(args), o...  11.2 us
    pallas_call x1, Pallas kernels, on_pair(): pl.pallas_call(finish, out_shape=[shaped(shape, dtype) for shape, dtype i...  2.9 us

profile of v5, /device:TPU:0, one launch (start us, length us, event | category | flops | bytes accessed | tf_op | source)
XLA Modules:
  0.0 14.7 jit_solution(5542026948961097881)
XLA Ops:
  0.6 11.2 %exchange.1 = (bf16[768,768]{1,0:T(8,128)(2,1)S(1)}, bf16[768]{0:T(1024)(128)(2,1)S(1)}, bf16[768]{0:T(1024)(128)(2,1)S(1)}, f32[384,768]{1,0:T(8,128)S(1)}, f32...) custom-call(f32[768,768]{1,0:T(8,128)} %bitcast.2, ...), custom_call_target="tpu_custom_call" | custom-call | tf_op jit(solution)/shard_map/exchange/pallas_call | solution.py:577
  11.8 2.9 %finish.1 = (bf16[768,768]{1,0:T(8,128)(2,1)}, bf16[768,768]{1,0:T(8,128)(2,1)}, bf16[768]{0:T(1024)(128)(2,1)}, bf16[768]{0:T(1024)(128)(2,1)}, f32[384,768]{1,...) custom-call(bf16[768,768]{1,0:T(8,128)(2,1)S(1)} %get-tuple-element., ...), custom_call_target="tpu_custom_call" | custom-call | tf_op jit(solution)/shard_map/finish/pallas_call | solution.py:613

commit v6 on v5

--- a/solution.py
+++ b/solution.py
@@ -124,14 +124,14 @@
     dma, regular = pltpu.SemaphoreType.DMA, pltpu.SemaphoreType.REGULAR
     pl.run_scoped(
         functools.partial(exchange_in_scope, *refs),
-        dma((2,)), dma((6,)), dma((groups + 7,)), dma((1,)), dma((groups + 2,)), dma((5,)), regular, regular,
+        dma((2,)), dma((7,)), dma((groups + 7,)), dma((1,)), dma((groups + 3,)), dma((5,)), regular, regular,
     )
 
 
 def exchange_in_scope(
     pu, pd, pn, pb, mu_h, md_h, mn, mb, eu_h, ed_h, en, eb,
     cu, cn, cb, su, sn, sb, tu, tn, tb,
-    pack, ed, stat_d, stat_m,
+    pack, ed, stat_d, stat_m, stat_o,
     own_u, own_d, give_u, sum_u, base_u, other_u, mu, md, eu,
     pn_v, pb_v, mn_v, mb_v, en_v, eb_v, vec, got_vec,
     sq_u, sq_o, acc_d, acc_o, stat_u, stat_w,
@@ -306,7 +306,6 @@
     wait_for(pack.at[pl.ds(0, 4)], load_sem.at[1])
     acc_d[...] = jnp.zeros_like(acc_d)
     acc_o[...] = jnp.zeros_like(acc_o)
-    stat_d[pl.ds(me * n + here, 1), 1:2, :] = jnp.zeros((1, 1, cols), jnp.float32)
 
     def eighths(x):
         return jnp.sum(x.reshape(x.shape[0] // 8, 8, cols), axis=0)
@@ -368,25 +367,26 @@
         sent[groups + at].wait_recv()
         sum_columns(span, acc_d, own_d, sum_d, sum_d)
 
-    def store_total(acc, which):
-        stat_d[pl.ds(slot_d, 1), which : which + 1, :] = jnp.sum(acc[...], axis=0).reshape(1, 1, cols)
+    def send_total():
+        stat_d[pl.ds(slot_d, 1), :, :] = jnp.sum(acc_d[...], axis=0).reshape(1, 1, cols)
+        sizes(stat_d, slot_d, 3, stat_sem.at[groups], 2)
 
     @pl.when(me == 0)
     def _():
-        store_total(acc_d, 0)
+        send_total()
 
     @pl.when(me == 1)
     def _():
         for at, span in enumerate(lasts):
             wait_for(sum_d.at[span, :], part_sem.at[groups + 3 + at])
             sum_columns(span, acc_d, own_d, sum_d, sum_d)
-        store_total(acc_d, 0)
+        send_total()
         for at, span in enumerate(lasts):
             wait_for(sum_d.at[span, :], part_sem.at[groups + 5 + at])
             sum_columns(span, acc_o, give_d, other_d.at[0])
-        store_total(acc_o, 1)
-
-    sizes(stat_d, slot_d, 3, stat_sem.at[groups], 2)
+        stat_o[pl.ds(here, 1), :, :] = jnp.sum(acc_o[...], axis=0).reshape(1, 1, cols)
+        sizes(stat_o, here, 6, stat_sem.at[groups + 2], 2)
+
 
     for group in range(groups):
         span = spans_u[group]
@@ -473,13 +473,23 @@
     wait_for(stat_m.at[pl.ds(0, 2 * n - 1)], small_sem.at[5])
     wait_for(stat_m.at[pl.ds(0, 2 * n - 1)], stat_sem.at[groups + 1])
     wait_for(stat_d.at[pl.ds(0, 2 * n - 1)], stat_sem.at[groups])
+
+    @pl.when(me == 0)
+    def _():
+        wait_for(stat_o, stat_sem.at[groups + 2])
+
+    @pl.when(me == 1)
+    def _():
+        wait_for(stat_o.at[pl.ds(0, n - 1)], stat_sem.at[groups + 2])
+        wait_for(stat_d.at[pl.ds(0, 2 * n - 1)], small_sem.at[6])
+
     wait_for(cu.at[at_core(peer, rows, 0, first), :], more_sem.at[3])
     wait_for(pack, send_sem.at[0])
 
 
 def finish(
     cu_v, cn_v, cb_v, su_v, sn_v, sb_v, tu_v, tn_v, tb_v,
-    pack, ed, stat_d, stat_m,
+    pack, ed, stat_d, stat_m, stat_o,
     cu, cd, cn, cb, su, sd, sn, sb, tu, td, tn, tb,
     cd_v, sd_v, td_v,
 ):
@@ -519,9 +529,8 @@
         for core in (me, 1 - me):
             weights = sizes = 0.0
             for at in range(n):
-                near, far = stat_d[core * n + at], stat_d[(1 - core) * n + at]
                 weights = weights + stat_m[core * n + at]
-                sizes = sizes + near[0:1, :] + far[1:2, :]
+                sizes = sizes + stat_d[core * n + at] + jnp.where(core == 0, stat_o[at], 0.0)
             scales.append(scale_of(weights, sizes, rate))
         own, other = scales
         for piece in range(pieces):
@@ -571,8 +580,9 @@
         *(shaped(x.shape) for x in (mu, mn, mb)),
         shaped((5, *md.shape)),
         shaped(md.shape),
-        shaped((2 * n, 2, cols)),
         shaped((2 * n, 1, cols)),
+        shaped((2 * n, 1, cols)),
+        shaped((n, 1, cols)),
     ]
     results = pl.pallas_call(
         exchange,

time: 14.9 us -> 14.9 us (level)
  no operation moved by 1% of the time
where the time goes in v6:
time: 14.9 us; the launch traced here: 14.7 us
  Pallas kernels  14.1 us (95%)
  between operations  0.65 us (4%)
    pallas_call x1, Pallas kernels, on_pair(): pl.pallas_call(exchange, out_shape=between, in_specs=[hbm] * len(args), o...  11.2 us
    pallas_call x1, Pallas kernels, on_pair(): pl.pallas_call(finish, out_shape=[shaped(shape, dtype) for shape, dtype i...  2.9 us

profile of v6, /device:TPU:0, one launch (start us, length us, event | category | flops | bytes accessed | tf_op | source)
XLA Modules:
  0.0 14.7 jit_solution(14286539398416799062)
XLA Ops:
  0.6 11.2 %exchange.1 = (bf16[768,768]{1,0:T(8,128)(2,1)S(1)}, bf16[768]{0:T(1024)(128)(2,1)S(1)}, bf16[768]{0:T(1024)(128)(2,1)S(1)}, f32[384,768]{1,0:T(8,128)S(1)}, f32...) custom-call(f32[768,768]{1,0:T(8,128)} %bitcast.2, ...), custom_call_target="tpu_custom_call" | custom-call | tf_op jit(solution)/shard_map/exchange/pallas_call | solution.py:587
  11.8 2.9 %finish.1 = (bf16[768,768]{1,0:T(8,128)(2,1)}, bf16[768,768]{1,0:T(8,128)(2,1)}, bf16[768]{0:T(1024)(128)(2,1)}, bf16[768]{0:T(1024)(128)(2,1)}, f32[384,768]{1,...) custom-call(bf16[768,768]{1,0:T(8,128)(2,1)S(1)} %get-tuple-element., ...), custom_call_target="tpu_custom_call" | custom-call | tf_op jit(solution)/shard_map/finish/pallas_call | solution.py:623

commit v7 on v6

--- a/solution.py
+++ b/solution.py
@@ -472,6 +472,8 @@
     wait_for(stat_d.at[pl.ds(0, 2 * n - 1)], small_sem.at[3])
     wait_for(stat_m.at[pl.ds(0, 2 * n - 1)], small_sem.at[5])
     wait_for(stat_m.at[pl.ds(0, 2 * n - 1)], stat_sem.at[groups + 1])
+    wait_for(cu.at[at_core(peer, rows, 0, first), :], more_sem.at[3])
+    wait_for(pack, send_sem.at[0])
     wait_for(stat_d.at[pl.ds(0, 2 * n - 1)], stat_sem.at[groups])
 
     @pl.when(me == 0)
@@ -482,9 +484,6 @@
     def _():
         wait_for(stat_o.at[pl.ds(0, n - 1)], stat_sem.at[groups + 2])
         wait_for(stat_d.at[pl.ds(0, 2 * n - 1)], small_sem.at[6])
-
-    wait_for(cu.at[at_core(peer, rows, 0, first), :], more_sem.at[3])
-    wait_for(pack, send_sem.at[0])
 
 
 def finish(

time: 14.9 us -> 14.9 us (level)
  no operation moved by 1% of the time
where the time goes in v7:
time: 14.9 us; the launch traced here: 14.7 us
  Pallas kernels  14.1 us (95%)
  between operations  0.65 us (4%)
    pallas_call x1, Pallas kernels, on_pair(): pl.pallas_call(exchange, out_shape=between, in_specs=[hbm] * len(args), o...  11.2 us
    pallas_call x1, Pallas kernels, on_pair(): pl.pallas_call(finish, out_shape=[shaped(shape, dtype) for shape, dtype i...  2.9 us

profile of v7, /device:TPU:0, one launch (start us, length us, event | category | flops | bytes accessed | tf_op | source)
XLA Modules:
  0.0 14.7 jit_solution(16077416245326860645)
XLA Ops:
  0.6 11.2 %exchange.1 = (bf16[768,768]{1,0:T(8,128)(2,1)S(1)}, bf16[768]{0:T(1024)(128)(2,1)S(1)}, bf16[768]{0:T(1024)(128)(2,1)S(1)}, f32[384,768]{1,0:T(8,128)S(1)}, f32...) custom-call(f32[768,768]{1,0:T(8,128)} %bitcast.2, ...), custom_call_target="tpu_custom_call" | custom-call | tf_op jit(solution)/shard_map/exchange/pallas_call | solution.py:586
  11.8 2.9 %finish.1 = (bf16[768,768]{1,0:T(8,128)(2,1)}, bf16[768,768]{1,0:T(8,128)(2,1)}, bf16[768]{0:T(1024)(128)(2,1)}, bf16[768]{0:T(1024)(128)(2,1)}, f32[384,768]{1,...) custom-call(bf16[768,768]{1,0:T(8,128)(2,1)S(1)} %get-tuple-element., ...), custom_call_target="tpu_custom_call" | custom-call | tf_op jit(solution)/shard_map/finish/pallas_call | solution.py:622
